TPU v7x, 256 devices: a whole 4x4x8 slice. The times are simulated.
256 devices in a mesh: band: 32 (over z, y_hi, core), chan: 8 (over x, y_lo).
Axes of the slice: x: 4, y: 4 (y_hi: 2, y_lo: 2; y = y_hi * 2 + y_lo), z: 8, core: 2. Of those that a mesh axis runs over, the one named last changes fastest.
Arguments:
- fine_features: bfloat16 [2, 192, 256, 512], P(None, 'chan', 'band'), may hold values from -100 to 100
- coarse_level: bfloat16 [2, 256, 128, 256], P(None, 'chan', 'band'), may hold values from -100 to 100
- lat_weight: bfloat16 [256, 192], P('chan'), may hold values from -0.4375 to 0.4375
- lat_gain: bfloat16 [256], P('chan'), may hold values from 0.099609375 to 1.8984375
- lat_shift: bfloat16 [256], P('chan'), may hold values from -3 to 3
- out_weight: bfloat16 [3, 3, 256, 256], P(None, None, 'chan'), may hold values from -0.125 to 0.125
- out_gain: bfloat16 [256], P('chan'), may hold values from 0.099609375 to 1.8984375
- out_shift: bfloat16 [256], P('chan'), may hold values from -3 to 3
- mask_weight: bfloat16 [256, 256], P('chan'), may hold values from -0.375 to 0.375
- mask_bias: bfloat16 [256], P('chan'), may hold values from -1.796875 to 1.796875
- queries: bfloat16 [200, 256], replicated, may hold values from -128 to 128
Outputs:
- log_probs: float32 [2, 200, 256, 512], P(None, None, ('band', 'chan'))
All inputs are finite; a program needn't handle non-finite values.
Results may differ from a plain program's by a relative error of at most 0.0058.
Values may be sent and summed in bfloat16 or wider, within the bound.
A program may use at most 64 MiB of HBM per device.

v0:
```python
import functools

import jax
import jax.numpy as jnp
from jax import lax
from jax.sharding import Mesh
from jax.sharding import PartitionSpec as P

D = 256
GROUPS = 32
BAND = ("band_0", "band_1", "band_2")
CHAN = ("chan_0", "chan_1")
BAND_CHAN = ("band_0", "band_1", "band_2", "chan_0", "chan_1")


epsilon = 1e-05


def whole_of(shard, axes, dim):
    for axis in reversed(axes):
        shard = lax.all_gather(shard, axis, axis=dim, tiled=True)
    return shard


def from_everyone(shard, axis):
    devices = lax.axis_size(axis)
    return lax.all_to_all(
        jnp.broadcast_to(shard[None], (devices, *shard.shape)), axis, 0, 0, tiled=True
    )


def of_everyone(shard, axis):
    everything = from_everyone(shard, axis)
    return jnp.sum(everything, axis=0)


def together(arrays, axis):
    vector, at, done = (jnp.concatenate([a.reshape(-1) for a in arrays]), 0, [])
    total = of_everyone(vector, axis)
    for a in arrays:
        done.append(total[at : at + a.size].reshape(a.shape))
        at += a.size
    return tuple(done)


def extended_2(cells, sides, width):
    for axis, dim in sides:
        count = lax.axis_size(axis)
        ends = count - 1
        head = lax.slice_in_dim(cells, 0, width, axis=dim)
        tail = lax.slice_in_dim(cells, cells.shape[dim] - width, cells.shape[dim], axis=dim)
        cells = jnp.concatenate(
            [
                lax.ppermute(tail, axis, [(i, (i + 1) % count) for i in range(ends)]),
                cells,
                lax.ppermute(head, axis, [((i + 1) % count, i) for i in range(ends)]),
            ],
            axis=dim,
        )
    return cells


def rows_first(arrays, axis, dims):
    turned = [jnp.moveaxis(a, dim, 0) for a, dim in zip(arrays, dims)]
    both = jnp.concatenate([t.reshape(len(t), -1) for t in turned], axis=1)
    result, at, done = (lax.all_gather(both, axis, axis=0, tiled=True), 0, [])
    for t, dim in zip(turned, dims):
        slab = result[:, at : at + t[0].size].reshape(-1, *t.shape[1:])
        done.append(jnp.moveaxis(slab, 0, dim))
        at += t[0].size
    return tuple(done)


def extended_3(shard, sides, width):
    edges = {}
    for axis, dim in sides:
        devices, length = (lax.axis_size(axis), shard.shape[dim])
        up = [(i, (i + 1) % devices) for i in range(devices - 1)]
        last = lax.slice_in_dim(shard, length - width, length, axis=dim)
        first = lax.slice_in_dim(shard, 0, width, axis=dim)
        edges[dim] = (
            lax.ppermute(last, axis, up),
            lax.ppermute(first, axis, [(b, a) for a, b in up]),
        )
    done = []
    for _, dim in sides:
        low, high = edges[dim]
        around = [(width, width) if d in done else (0, 0) for d in range(shard.ndim)]
        shard = jnp.concatenate([jnp.pad(low, around), shard, jnp.pad(high, around)], axis=dim)
        done.append(dim)
    return shard


def over_axes_2(shard, axes):
    return functools.reduce(lax.psum, axes, shard)


def interp(padded, axis):
    length = padded.shape[axis] - 2
    before = lax.slice_in_dim(padded, 0, length, axis=axis)
    middle = lax.slice_in_dim(padded, 1, length + 1, axis=axis)
    after = lax.slice_in_dim(padded, 2, length + 2, axis=axis)
    even_part = 0.25 * before + 0.75 * middle
    odd_part = 0.75 * middle + 0.25 * after
    paired = jnp.stack([even_part, odd_part], axis + 1)
    new_shape = list(middle.shape)
    new_shape[axis] = 2 * length
    return paired.reshape(new_shape)


def conv_taps(taps_weight, padded, row_count, col_count):
    summed = None
    for row_tap in range(3):
        for col_tap in range(3):
            window = padded[:, :, row_tap : row_tap + row_count, col_tap : col_tap + col_count]
            term = jnp.einsum(
                "oc,ncrw->norw",
                taps_weight[row_tap, col_tap],
                window,
                preferred_element_type=jnp.float32,
            )
            summed = term if summed is None else summed + term
    return summed


def apply_norm(blocks, mean_value, variance, full_shape, gain, shift):
    scaled = (
        (blocks - mean_value[:, :, None]) * lax.rsqrt(variance[:, :, None] + epsilon)
    ).reshape(full_shape)
    return (
        scaled * gain.astype(jnp.float32)[None, :, None, None]
        + shift.astype(jnp.float32)[None, :, None, None]
    )


def per_device(
    fine_features,
    coarse_level,
    lat_weight,
    lat_gain,
    lat_shift,
    out_weight,
    out_gain,
    out_shift,
    mask_weight,
    mask_bias,
    queries,
):
    images, in_share, band_rows, columns = fine_features.shape
    out_share = lat_weight.shape[0]
    group_size = D // GROUPS
    band_count = lax.axis_size(BAND)
    pixel_count = float(group_size * band_rows * band_count * columns)
    lateral = jnp.einsum(
        "oc,ncrw->norw",
        lat_weight,
        whole_of(fine_features, CHAN, 1),
        preferred_element_type=jnp.float32,
    )
    lat_blocks = lateral.reshape(images, out_share // group_size, -1)
    first_sum, square_sum = together(
        (jnp.sum(lat_blocks, 2), jnp.sum(lat_blocks * lat_blocks, 2)), BAND
    )
    lat_mean = first_sum / pixel_count
    lat_var = square_sum / pixel_count - lat_mean * lat_mean
    lat_normed = apply_norm(lat_blocks, lat_mean, lat_var, lateral.shape, lat_gain, lat_shift)
    band_index = lax.axis_index(BAND)
    extended = extended_2(coarse_level, ((BAND, 2),), 1)
    top_row = jnp.where(band_index == 0, extended[:, :, 1:2], extended[:, :, 0:1])
    bottom_row = jnp.where(band_index == band_count - 1, extended[:, :, -2:-1], extended[:, :, -1:])
    extended = jnp.concatenate([top_row, extended[:, :, 1:-1], bottom_row], 2).astype(jnp.float32)
    extended = jnp.pad(extended, ((0, 0), (0, 0), (0, 0), (1, 1)), mode="edge")
    upsampled = interp(interp(extended, 2), 3)
    joined = (lat_normed + upsampled).astype(jnp.bfloat16)
    row_joined = lax.all_to_all(joined, CHAN, split_axis=2, concat_axis=1, tiled=True)
    conv_weight, full_gain, full_shift, full_mask, full_bias = rows_first(
        (out_weight, out_gain, out_shift, mask_weight, mask_bias), CHAN, (2, 0, 0, 0, 0)
    )
    row_count = row_joined.shape[2]
    padded = extended_3(row_joined, ((BAND_CHAN, 2),), 1)
    padded = jnp.pad(padded, ((0, 0), (0, 0), (0, 0), (1, 1)))
    conv_out = conv_taps(conv_weight, padded, row_count, columns)
    local_groups = conv_out.shape[1] // group_size
    conv_blocks = conv_out.reshape(images, local_groups, -1)
    first_sum, square_sum = (
        over_axes_2(jnp.sum(conv_blocks, 2), BAND_CHAN),
        over_axes_2(jnp.sum(conv_blocks * conv_blocks, 2), BAND_CHAN),
    )
    out_mean = first_sum / pixel_count
    out_var = square_sum / pixel_count - out_mean * out_mean
    activated = jnp.maximum(
        apply_norm(conv_blocks, out_mean, out_var, conv_out.shape, full_gain, full_shift), 0.0
    ).astype(jnp.bfloat16)
    mixed = jnp.einsum("oc,ncrw->norw", full_mask, activated, preferred_element_type=jnp.float32)
    features = (mixed + full_bias.astype(jnp.float32)[None, :, None, None]).astype(jnp.bfloat16)
    logits = jnp.einsum("qc,ncrw->nqrw", queries, features, preferred_element_type=jnp.float32)
    peak = jnp.max(logits, axis=1, keepdims=True)
    shifted = logits - peak
    return shifted - jnp.log(jnp.sum(jnp.exp(shifted), axis=1, keepdims=True))


def solution(mesh):
    finer = Mesh(
        mesh.devices.reshape(8, 2, 2, 4, 2), ("band_0", "band_1", "band_2", "chan_0", "chan_1")
    )
    return jax.shard_map(
        per_device,
        mesh=finer,
        in_specs=(
            P(None, CHAN, BAND, None),
            P(None, CHAN, BAND, None),
            P(CHAN, None),
            P(CHAN),
            P(CHAN),
            P(None, None, CHAN, None),
            P(CHAN),
            P(CHAN),
            P(CHAN, None),
            P(CHAN),
            P(),
        ),
        out_specs=P(None, None, BAND_CHAN, None),
        check_vma=False,
    )
```

profile of v0, /device:TPU:1, one launch (start us, length us, event | category | flops | bytes accessed | tf_op | source)
XLA Modules:
  0.0 194.1 jit_solution(14821775544528148993)
XLA Ops:
  6.6 1.3 copy.111
  7.9 10.6 %all_gather.9 = bf16[2,48,8,512]{3,1,2,0:T(8,128)(2,1)} all-gather(bf16[2,24,8,512]{3,1,2,0:T(8,128)(2,1)S(1)} %copy.111), channel_id=1, replica_groups=mesh['band_0'=8,'band_1'=2,'band_2'=2,'chan_0'=4,'chan_1'=2] {'chan_1'}, dimensions={1}, use_global_device_ids=true | all-gather | bytes 1179648 | tf_op jit(solution)/shard_map/all_gather | solution.py:21
  18.6 7.4 %collective-permute-start = (bf16[2,32,1,256]{3,1,2,0:T(8,128)(2,1)S(1)}, bf16[2,32,1,256]{3,1,2,0:T(8,128)(2,1)S(1)}, u32[]{:S(2)}, u32[]{:S(2)}) collective-permute-start(bf16[2,32,1,256]{3,1,2,0:T(8,128)(2,1)S(1)} %get-tuple-element.30), channel_id=1, source_target_pairs={{0,8},{8,16},{16,24},{24,32},{32,40},{40,48},{48,56},{56,64},{64,7... | collective-permute-start | bytes 98312 | tf_op jit(solution)/shard_map/ppermute | solution.py:54
  26.0 1.9 collective-permute-start.1
  27.9 0.1 copy.127
  28.0 0.1 copy.128
  28.1 0.1 copy.129
  28.2 0.1 copy.126
  28.4 0.2 reshape.197
  28.6 0.8 concatenate.20
  29.4 3.3 %collective-permute-done.1 = bf16[2,32,1,256]{3,1,2,0:T(8,128)(2,1)S(1)} collective-permute-done((bf16[2,32,1,256]{3,1,2,0:T(8,128)(2,1)S(1)}, bf16[2,32,1,256]{3,1,2,0:T(8,128)(2,1)S(1)}, u32[]{:S(2)}, u32[]{:S(2)}) %collective-permute-start.1) | collective-permute-done | bytes 32800 | tf_op jit(solution)/shard_map/ppermute | solution.py:56
  32.8 0.1 fusion.51
  32.9 0.3 pad_maximum_fusion.2
  33.2 0.1 fusion.43
  33.4 0.3 fusion.24
  33.7 31.8 %all-gather.3.cloned.1.call-done = bf16[2,192,8,512]{3,1,2,0:T(8,128)(2,1)} async-done(((bf16[2,48,8,512]{3,1,2,0:T(8,128)(2,1)}), bf16[2,192,8,512]{3,1,2,0:T(8,128)(2,1)}) %all-gather.3.cloned.1.call-update) | async-done | bytes 3145744 | tf_op jit(solution)/shard_map/all_gather | solution.py:21
  65.5 2.7 %fusion.50 = (f32[2,32]{1,0:T(2,128)S(1)}, f32[2,32]{1,0:T(2,128)S(1)}, f32[2,32,8,512]{3,1,2,0:T(8,128)S(1)}) fusion(bf16[2,192,8,512]{3,1,2,0:T(8,128)(2,1)} %all-gather.3.cloned.1.call-done, bf16[32,192]{1,0:T(8,128)(2,1)S(1)} %copy-done.5), kind=kOutput, calls=%fused_computation.91 | convolution fusion | flops 101449600 | bytes 4207104 | tf_op jit(solution)/shard_map/oc,ncrw->norw/dot_general | solution.py:154
  68.2 0.1 reduce_sum.67
  68.5 0.1 reduce_sum.73
  68.7 0.6 broadcast_in_dim.2
  69.4 10.5 %all-to-all-start = ((f32[32,1,16]{2,1,0:T(1,128)}), f32[32,1,16]{2,1,0:T(1,128)S(1)}, u32[]{:S(2)}, u32[]{:S(2)}) async-start(f32[32,1,16]{2,1,0:T(1,128)} %broadcast_in_dim.2), calls=%async_computation | async-start | bytes 32768 | tf_op jit(solution)/shard_map/all_to_all | solution.py:27
  79.8 0.1 pad_maximum_fusion
  79.9 3.7 %copy.119 = f32[2,32,8,256,2]{1,2,4,3,0:T(8,128)} copy(f32[2,32,8,256,2]{3,1,2,0,4:T(8,128)S(1)} %pad_maximum_fusion) | data formatting | bytes 2097152 | tf_op jit(solution)/shard_map/stack | solution.py:105
  83.6 2.8 %copy.120 = f32[2,32,8,512]{3,1,2,0:T(8,128)S(1)} copy(f32[2,32,8,512]{1,2,3,0:T(8,128)} %bitcast.154) | data formatting | bytes 2097152 | tf_op jit(solution)/shard_map/reshape | solution.py:108
  86.4 2.7 %all-to-all-done = f32[32,1,16]{2,1,0:T(1,128)S(1)} async-done(((f32[32,1,16]{2,1,0:T(1,128)}), f32[32,1,16]{2,1,0:T(1,128)S(1)}, u32[]{:S(2)}, u32[]{:S(2)}) %all-to-all-start) | async-done | bytes 2080 | tf_op jit(solution)/shard_map/all_to_all | solution.py:27
  89.5 0.1 sub.54
  89.7 0.1 mul.92
  89.8 0.4 add_convert_fusion
  90.2 14.5 %all_to_all.24 = bf16[2,32,8,512]{3,1,0,2:T(8,128)(2,1)S(1)} all-to-all(bf16[2,32,8,512]{3,1,0,2:T(8,128)(2,1)S(1)} %copy.121), channel_id=1, replica_groups=mesh['band_0'=8,'band_1'=2,'band_2'=2,'chan_0'=4,'chan_1'=2] {'chan_0','..., dimensions={2} | all-to-all | bytes 1048576 | tf_op jit(solution)/shard_map/all_to_all | solution.py:175
  104.7 1.0 copy.123
  105.7 4.7 %collective-permute-start.3 = (bf16[2,256,1,512]{1,3,0,2:T(8,128)(2,1)}, bf16[2,256,1,512]{1,3,0,2:T(8,128)(2,1)}, u32[]{:S(2)}, u32[]{:S(2)}) collective-permute-start(bf16[2,256,1,512]{1,3,0,2:T(8,128)(2,1)} %copy.123), channel_id=1, source_target_pairs={{1,0},{2,1},{3,2},{4,3},{5,4},{6,5},{7,6},{8,7},{9,8},{10,9},{11,1... | collective-permute-start | bytes 1572872 | tf_op jit(solution)/shard_map/ppermute | solution.py:83
  110.5 1.9 collective-permute-start.2
  112.4 12.1 %all-gather.5.cloned.1.call-done = bf16[256,2563]{1,0:T(8,128)(2,1)} async-done(((bf16[32,2563]{1,0:T(8,128)(2,1)}), bf16[256,2563]{1,0:T(8,128)(2,1)}) %all-gather.5.cloned.1.call-update) | async-done | bytes 1312272 | tf_op jit(solution)/shard_map/all_gather | solution.py:66
  124.5 1.3 slice-done
  125.7 0.6 copy.130
  126.3 1.6 copy.131
  127.9 0.2 convert_reduce_fusion.2
  128.1 1.3 fusion.44
  129.4 1.9 collective-permute-done.3
  131.2 4.4 %collective-permute-done.2 = bf16[2,256,1,512]{1,3,0,2:T(8,128)(2,1)} collective-permute-done((bf16[2,256,1,512]{1,3,0,2:T(8,128)(2,1)}, bf16[2,256,1,512]{1,3,0,2:T(8,128)(2,1)}, u32[]{:S(2)}, u32[]{:S(2)}) %collective-permute-start.2) | collective-permute-done | bytes 524320 | tf_op jit(solution)/shard_map/ppermute | solution.py:82
  135.6 1.7 fusion.5
  137.4 0.3 fusion.17
  137.7 0.3 fusion.18
  138.0 0.3 fusion.19
  138.4 0.3 fusion.20
  138.7 0.3 fusion.16
  139.1 1.4 fusion.27
  140.4 1.4 fusion.25
  141.8 1.6 fusion.49
  143.5 0.1 reduce_sum.90
  143.5 0.1 reduce_sum.91
  143.6 0.1 reduce_sum.93
  143.7 0.1 reduce_sum.94
  143.8 14.1 %all-reduce.1 = (f32[2,32]{1,0:T(2,128)S(1)}, f32[2,32]{1,0:T(2,128)S(1)}) all-reduce(f32[2,32]{1,0:T(2,128)S(1)} %reduce_sum.94, f32[2,32]{1,0:T(2,128)S(1)} %reduce_sum.91), channel_id=1, replica_groups=mesh['band_0'=8,'band_1'=2,'band_2'=2,'chan_0'=4,'chan_1'=2] {'band_0'}, use_global_device_ids=true, to_apply=%region_14.15 | all-reduce | flops 128 | bytes 1024 | tf_op jit(solution)/shard_map/psum | solution.py:95
  158.0 5.3 %all-reduce.5 = (f32[2,32]{1,0:T(2,128)S(1)}, f32[2,32]{1,0:T(2,128)S(1)}) all-reduce(f32[2,32]{1,0:T(2,128)S(1)} %get-tuple-element.12, f32[2,32]{1,0:T(2,128)S(1)} %get-tuple-element.13), channel_id=1, replica_groups=mesh['band_0'=8,'band_1'=2,'band_2'=2,'chan_0'=4,'chan_1'=2] {'band_1'}, use_global_device_ids=true, to_apply=%region_15.16 | all-reduce | flops 128 | bytes 1024 | tf_op jit(solution)/shard_map/psum | solution.py:95
  163.2 7.2 %all-reduce.4 = (f32[2,32]{1,0:T(2,128)S(1)}, f32[2,32]{1,0:T(2,128)S(1)}) all-reduce(f32[2,32]{1,0:T(2,128)S(1)} %get-tuple-element.20, f32[2,32]{1,0:T(2,128)S(1)} %get-tuple-element.21), channel_id=1, replica_groups=mesh['band_0'=8,'band_1'=2,'band_2'=2,'chan_0'=4,'chan_1'=2] {'band_2'}, use_global_device_ids=true, to_apply=%region_16.17 | all-reduce | flops 128 | bytes 1024 | tf_op jit(solution)/shard_map/psum | solution.py:95
  170.4 8.8 %all-reduce.2 = (f32[2,32]{1,0:T(2,128)S(1)}, f32[2,32]{1,0:T(2,128)S(1)}) all-reduce(f32[2,32]{1,0:T(2,128)S(1)} %get-tuple-element.18, f32[2,32]{1,0:T(2,128)S(1)} %get-tuple-element.19), channel_id=1, replica_groups=mesh['band_0'=8,'band_1'=2,'band_2'=2,'chan_0'=4,'chan_1'=2] {'chan_0'}, use_global_device_ids=true, to_apply=%region_17.18 | all-reduce | flops 128 | bytes 1024 | tf_op jit(solution)/shard_map/psum | solution.py:95
  179.2 3.8 %all-reduce.3 = (f32[2,32]{1,0:T(2,128)S(1)}, f32[2,32]{1,0:T(2,128)S(1)}) all-reduce(f32[2,32]{1,0:T(2,128)S(1)} %get-tuple-element.14, f32[2,32]{1,0:T(2,128)S(1)} %get-tuple-element.15), channel_id=1, replica_groups=mesh['band_0'=8,'band_1'=2,'band_2'=2,'chan_0'=4,'chan_1'=2] {'chan_1'}, use_global_device_ids=true, to_apply=%region_18.19 | all-reduce | flops 128 | bytes 1024 | tf_op jit(solution)/shard_map/psum | solution.py:95
  183.1 0.1 sub.59
  183.2 0.1 mul.108
  183.3 1.9 %fusion.53 = (f32[2,512]{1,0:T(2,128)S(1)}, f32[2,200,1,512]{3,1,0,2:T(8,128)S(1)}) fusion(bf16[200,256]{1,0:T(8,128)(2,1)S(1)} %copy-done, f32[2,256,1,512]{1,3,0,2:T(8,128)} %get-tuple-element.37, f32[256]{0:T(256)S(1)} %get-tuple-element.6, f32[256]{0:T(256)S(1)} %get-tuple-element.7, f32[256]{0:T(256)S(1)} %get-tuple-element.5, f32[2,256]{1,0:T(2,128)S(1)} %mul.108, ...), kind=kOutput, calls=%fused_computation.94 | convolution fusion | flops 241376256 | bytes 2112512 | tf_op jit(solution)/shard_map/qc,ncrw->nqrw/dot_general | solution.py:196
  185.3 0.1 exponential_reduce_fusion
  185.4 0.1 subtract_subtract_fusion
  185.6 1.7 copy.134
  (55 shorter events, 1.4 us)
Async XLA Ops:
  6.5 176.8 %copy-start = (bf16[200,256]{1,0:T(8,128)(2,1)S(1)}, bf16[200,256]{1,0:T(8,128)(2,1)}, u32[]{:S(2)}) copy-start(bf16[200,256]{1,0:T(8,128)(2,1)} %param.21) | copy-start | bytes 307204
  6.5 12.0 %copy-start.4 = (bf16[2,32,4,256]{3,2,1,0:T(4,128)(2,1)S(1)}, bf16[2,32,4,256]{3,2,1,0:T(4,128)(2,1)}, u32[]{:S(2)}) copy-start(bf16[2,32,4,256]{3,2,1,0:T(4,128)(2,1)} %param.12) | copy-start | bytes 393220
  6.5 21.4 %copy-start.7 = (bf16[32]{0:T(256)(128)(2,1)S(1)}, bf16[32]{0:T(256)(128)(2,1)}, u32[]{:S(2)}) copy-start(bf16[32]{0:T(256)(128)(2,1)} %param.17) | copy-start | bytes 196
  6.5 21.5 %copy-start.8 = (bf16[32]{0:T(256)(128)(2,1)S(1)}, bf16[32]{0:T(256)(128)(2,1)}, u32[]{:S(2)}) copy-start(bf16[32]{0:T(256)(128)(2,1)} %param.18) | copy-start | bytes 196
  6.5 21.6 %copy-start.9 = (bf16[32]{0:T(256)(128)(2,1)S(1)}, bf16[32]{0:T(256)(128)(2,1)}, u32[]{:S(2)}) copy-start(bf16[32]{0:T(256)(128)(2,1)} %param.20) | copy-start | bytes 196
  6.5 21.7 %copy-start.3 = (bf16[3,3,32,256]{3,2,1,0:T(8,128)(2,1)S(1)}, bf16[3,3,32,256]{3,2,1,0:T(8,128)(2,1)}, u32[]{:S(2)}) copy-start(bf16[3,3,32,256]{3,2,1,0:T(8,128)(2,1)} %param.16) | copy-start | bytes 442372
  6.6 58.9 %all-gather.3.cloned.1.call-start = ((), (), s32[]{:S(2)}) async-start(), calls=%async_computation.2 | async-start | bytes 3932160 | tf_op jit(solution)/shard_map/all_gather | solution.py:21
  7.9 20.7 %copy-start.6 = (bf16[32,256]{1,0:T(8,128)(2,1)S(1)}, bf16[32,256]{1,0:T(8,128)(2,1)}, u32[]{:S(2)}) copy-start(bf16[32,256]{1,0:T(8,128)(2,1)} %param.19) | copy-start | bytes 49156
  7.9 21.5 %copy-start.10 = (bf16[32]{0:T(256)(128)(2,1)S(1)}, bf16[32]{0:T(256)(128)(2,1)}, u32[]{:S(2)}) copy-start(bf16[32]{0:T(256)(128)(2,1)} %param.14) | copy-start | bytes 196
  7.9 21.5 %copy-start.11 = (bf16[32]{0:T(256)(128)(2,1)S(1)}, bf16[32]{0:T(256)(128)(2,1)}, u32[]{:S(2)}) copy-start(bf16[32]{0:T(256)(128)(2,1)} %param.15) | copy-start | bytes 196
  18.5 105.9 %all-gather.5.cloned.1.call-start = ((), (), s32[]{:S(2)}) async-start(), calls=%async_computation.3 | async-start | bytes 1548288 | tf_op jit(solution)/shard_map/all_gather | solution.py:66
  18.6 10.8 %collective-permute-start = (bf16[2,32,1,256]{3,1,2,0:T(8,128)(2,1)S(1)}, bf16[2,32,1,256]{3,1,2,0:T(8,128)(2,1)S(1)}, u32[]{:S(2)}, u32[]{:S(2)}) collective-permute-start(bf16[2,32,1,256]{3,1,2,0:T(8,128)(2,1)S(1)} %get-tuple-element.30), channel_id=1, source_target_pairs={{0,8},{8,16},{16,24},{24,32},{32,40},{40,48},{48,56},{56,64},{64,7... | collective-permute-start | bytes 98312 | tf_op jit(solution)/shard_map/ppermute | solution.py:54
  26.0 6.7 %collective-permute-start.1 = (bf16[2,32,1,256]{3,1,2,0:T(8,128)(2,1)S(1)}, bf16[2,32,1,256]{3,1,2,0:T(8,128)(2,1)S(1)}, u32[]{:S(2)}, u32[]{:S(2)}) collective-permute-start(bf16[2,32,1,256]{3,1,2,0:T(8,128)(2,1)S(1)} %get-tuple-element.31), channel_id=1, source_target_pairs={{8,0},{16,8},{24,16},{32,24},{40,32},{48,40},{56,48},{64,56},{72,6... | collective-permute-start | bytes 98312 | tf_op jit(solution)/shard_map/ppermute | solution.py:56
  33.3 32.1 %copy-start.5 = (bf16[32,192]{1,0:T(8,128)(2,1)S(1)}, bf16[32,192]{1,0:T(8,128)(2,1)}, u32[]{:S(2)}) copy-start(bf16[32,192]{1,0:T(8,128)(2,1)} %param.13) | copy-start | bytes 36868
  69.4 19.8 %all-to-all-start = ((f32[32,1,16]{2,1,0:T(1,128)}), f32[32,1,16]{2,1,0:T(1,128)S(1)}, u32[]{:S(2)}, u32[]{:S(2)}) async-start(f32[32,1,16]{2,1,0:T(1,128)} %broadcast_in_dim.2), calls=%async_computation | async-start | bytes 32768 | tf_op jit(solution)/shard_map/all_to_all | solution.py:27
  105.7 25.5 %collective-permute-start.3 = (bf16[2,256,1,512]{1,3,0,2:T(8,128)(2,1)}, bf16[2,256,1,512]{1,3,0,2:T(8,128)(2,1)}, u32[]{:S(2)}, u32[]{:S(2)}) collective-permute-start(bf16[2,256,1,512]{1,3,0,2:T(8,128)(2,1)} %copy.123), channel_id=1, source_target_pairs={{1,0},{2,1},{3,2},{4,3},{5,4},{6,5},{7,6},{8,7},{9,8},{10,9},{11,1... | collective-permute-start | bytes 1572872 | tf_op jit(solution)/shard_map/ppermute | solution.py:83
  110.5 25.2 %collective-permute-start.2 = (bf16[2,256,1,512]{1,3,0,2:T(8,128)(2,1)}, bf16[2,256,1,512]{1,3,0,2:T(8,128)(2,1)}, u32[]{:S(2)}, u32[]{:S(2)}) collective-permute-start(bf16[2,256,1,512]{1,3,0,2:T(8,128)(2,1)} %copy.123), channel_id=1, source_target_pairs={{0,1},{1,2},{2,3},{3,4},{4,5},{5,6},{6,7},{7,8},{8,9},{9,10},{10,1... | collective-permute-start | bytes 1572872 | tf_op jit(solution)/shard_map/ppermute | solution.py:82
  124.4 1.3 slice-start
  126.3 1.6 copy-start.1
  129.4 8.0 %copy-start.2 = (bf16[256,3,3,256]{3,0,2,1:T(8,128)(2,1)S(1)}, bf16[256,3,3,256]{3,0,2,1:T(8,128)(2,1)}, u32[]{:S(2)}) copy-start(bf16[256,3,3,256]{3,0,2,1:T(8,128)(2,1)} %copy.131) | copy-start | bytes 3538948
Sparse Core Ops, SparseCore 0:
  18.6 46.7 all-gather.2
  67.3 57.1 all-gather.4
where the time goes:
time: 196 us; the launch traced here: 194 us
  blocking collectives  64.3 us (33%)
  waiting for transfers between devices  56.2 us (29%)
  starting transfers between devices  26.5 us (14%)
  local copies, waits for them, and re-layouts  17.5 us (9%)
  between operations  13.8 us (7%)
  matrix products  11.9 us (6%)
  other arithmetic  4.01 us (2%)
    psum x5, blocking collectives, over_axes_2(): return functools.reduce(lax.psum, axes, shard)  39.2 us
    all_gather x1, waiting for transfers between devices, whole_of(): shard = lax.all_gather(shard, axis, axis=dim, tiled=True)  31.8 us
    all_to_all x1, blocking collectives, per_device(): lax.all_to_all(joined, CHAN, split_axis=2, concat_axis=1, tiled=True)  14.5 us
    all_gather x1, waiting for transfers between devices, rows_first(): result, at, done = (lax.all_gather(both, axis, axis=0, tiled=True), 0, [])  12.1 us
    all_gather x1, blocking collectives, whole_of(): shard = lax.all_gather(shard, axis, axis=dim, tiled=True)  10.6 us
    all_to_all x1, starting transfers between devices, from_everyone(): lax.all_to_all(jnp.broadcast_to(shard[None], (devices, *shard.shape)), ax...  10.5 us
    ppermute x1, starting transfers between devices, extended_2(): lax.ppermute(tail, axis, [(i, (i + 1) % count) for i in range(ends)])  7.37 us
    dot_general x9, matrix products, conv_taps(): jnp.einsum('oc,ncrw->norw', taps_weight[row_tap, col_tap], window, prefer...  7.3 us
  transfers between devices with their start and end apart: 7, of which 6 were waited for; matrix products, arithmetic and copies ran while one was open for 9% of the time, Pallas kernels for 0%

commit v1 on v0

v1 whole, which is shorter than its diff:
```python
import functools

import jax
import jax.numpy as jnp
from jax import lax
from jax.experimental import pallas as pl
from jax.experimental.pallas import tpu as pltpu
from jax.sharding import Mesh
from jax.sharding import PartitionSpec as P

D = 256
GROUPS = 32
COLS = 512
AXES = ("band_0", "band_1", "band_2", "chan_0", "chan_1")
BAND = AXES[:3]
CHAN = AXES[3:]
MESH = pl.DeviceIdType.MESH
f32, bf16 = jnp.float32, jnp.bfloat16
epsilon = 1e-05

CHAN_OFF = [(dx, dy) for dx in (1, 3, 2, 0) for dy in (0, 1) if (dx, dy) != (0, 0)]
PLANE_OFF = [
    (dx, dh, dl)
    for dx in (2, 1, 3, 0)
    for dh in (1, 0)
    for dl in (1, 0)
    if (dx, dh, dl) != (0, 0, 0)
]
LINE_OFF = [(dz, dc) for dz in (4, 3, 5, 2, 6, 1, 7, 0) for dc in (1, 0) if (dz, dc) != (0, 0)]


def kernel(
    pixels,
    fine, coarse, latw, lat_gain, lat_shift, outw, out_gain, out_shift, maskw, mask_bias, queries,
    out,
    X, C, WL, WC, PB, pstage, LAT, UPS, JS, CO, RC,
    plane_src, plane_dst, line_src, line_dst,
    s_fine, r_fine, s_coarse, r_coarse, s_latw, r_latw, s_par, r_par, s_w, r_w, s_m, r_m,
    s_halo, r_halo, s_core, r_core, s_plane, r_plane, s_line, r_line, s_row, r_row,
):
    z, yh, core = (lax.axis_index(a) for a in BAND)
    x, yl = (lax.axis_index(a) for a in CHAN)
    me = x * 2 + yl
    pair = ((z * 2 + yh) * 2 + core) * 4 + x

    def chan_peer(dx, dy):
        return (z, yh, core, lax.rem(x + dx, 4), lax.rem(yl + dy, 2))

    def plane_peer(dx, dh, dl):
        return (z, lax.rem(yh + dh, 2), core, lax.rem(x + dx, 4), lax.rem(yl + dl, 2))

    def line_peer(dz, dc):
        return (lax.rem(z + dz, 8), yh, lax.rem(core + dc, 2), x, yl)

    def pair_owner(g):
        b = lax.div(g, 4)
        return (lax.div(b, 4), lax.rem(lax.div(b, 2), 2), lax.rem(b, 2), lax.rem(g, 4), yl)

    above = pair_owner(lax.rem(pair + 127, 128))
    below = pair_owner(lax.rem(pair + 1, 128))
    partner = (z, yh, 1 - core, x, yl)
    other = (z, yh, core, x, 1 - yl)

    def remote(src, dst, send, recv, dev):
        return pltpu.make_async_remote_copy(
            src_ref=src, dst_ref=dst, send_sem=send, recv_sem=recv,
            device_id=dev, device_id_type=MESH,
        )

    barrier = pltpu.get_barrier_semaphore()
    for dev in [plane_peer(*o) for o in PLANE_OFF] + [line_peer(*o) for o in LINE_OFF] + [above, below]:
        pl.semaphore_signal(barrier, inc=1, device_id=dev, device_id_type=MESH)
    pstage[...] = jnp.zeros_like(pstage)
    for j, ref in enumerate((lat_gain, lat_shift, out_gain, out_shift, mask_bias)):
        pstage[j : j + 1, 0:32] = ref[...].astype(f32)
    PB[me] = pstage[...]
    WL[me] = latw[...]
    X[pl.ds(1, 2), me] = fine[yl, pl.ds(2 * x, 2)]
    C[1, me] = coarse[yl, x]
    WC[pl.ds(0, 9), me, core] = outw[:, core]
    WC[9, me, core] = maskw[core]
    pl.semaphore_wait(barrier, len(PLANE_OFF) + len(LINE_OFF) + 2)

    fine_c, coarse_c, latw_c, par_c, w_c, m_c = [], [], [], [], [], []
    for k, o in enumerate(CHAN_OFF):
        dev = chan_peer(*o)
        fine_c.append(remote(fine.at[dev[4], pl.ds(2 * dev[3], 2)], X.at[pl.ds(1, 2), me],
                             s_fine.at[k], r_fine.at[k], dev))
        latw_c.append(remote(latw, WL.at[me], s_latw.at[k], r_latw.at[k], dev))
        par_c.append(remote(pstage, PB.at[me], s_par.at[k], r_par.at[k], dev))
        coarse_c.append(remote(coarse.at[dev[4], dev[3]], C.at[1, me],
                               s_coarse.at[k], r_coarse.at[k], dev))
        w_c.append(remote(outw.at[:, core], WC.at[pl.ds(0, 9), me, core], s_w.at[k], r_w.at[k], dev))
        m_c.append(remote(maskw.at[core], WC.at[9, me, core], s_m.at[k], r_m.at[k], dev))
    for group in (latw_c, fine_c, par_c, coarse_c):
        for c in group:
            c.start()

    ci = lax.broadcasted_iota(jnp.int32, (256, COLS), 0)
    cj = lax.broadcasted_iota(jnp.int32, (256, COLS), 1)
    center = lax.shift_right_logical(cj, 1)
    side = jnp.clip(jnp.where(lax.bitwise_and(cj, 1) == 0, center - 1, center + 1), 0, 255)
    widen = (jnp.where(ci == center, 0.75, 0.0) + jnp.where(ci == side, 0.25, 0.0)).astype(bf16)

    def lateral_of(slot):
        rows = X[slot].astype(f32).reshape(192, COLS).astype(bf16)
        return jnp.dot(WL[...].astype(f32).reshape(256, 192).astype(bf16), rows,
                       preferred_element_type=f32)

    def row_stats(rows):
        s = q = None
        for row in rows:
            for k in range(COLS // 128):
                t = row[:, 128 * k : 128 * (k + 1)]
                s = t if s is None else s + t
                q = t * t if q is None else q + t * t
        both = jnp.concatenate(
            [jnp.sum(s.reshape(GROUPS, 8, 128), 1), jnp.sum(q.reshape(GROUPS, 8, 128), 1),
             jnp.zeros((64, 128), f32)], 0)
        return jnp.sum(jnp.transpose(both), 0, keepdims=True)

    def scale_shift(total, gain, shift):
        tall = jnp.transpose(jnp.broadcast_to(total, (128, 128)))
        mean = tall[0:32] / pixels
        var = tall[32:64] / pixels - mean * mean
        rstd = lax.rsqrt(var + epsilon)
        spread = lambda v: jnp.broadcast_to(v[:, None, :], (GROUPS, 8, 128)).reshape(D, 128)
        a = spread(rstd) * gain
        return a, shift - spread(mean) * a

    def send_plane(it, stats, offsets):
        plane_src[it] = stats
        done = []
        for k, o in enumerate(PLANE_OFF):
            if o in offsets:
                c = remote(plane_src.at[it], plane_dst.at[it, k], s_plane.at[it, k],
                           r_plane.at[it, k], plane_peer(*o))
                c.start()
                done.append(c)
        return done

    def send_line(it):
        done = []
        for k, o in enumerate(LINE_OFF):
            c = remote(line_src.at[it], line_dst.at[it, k], s_line.at[it, k],
                       r_line.at[it, k], line_peer(*o))
            c.start()
            done.append(c)
        return done

    def line_total(it):
        t = line_src[it]
        for k in range(len(LINE_OFF)):
            t = t + line_dst[it, k]
        return t

    for c in latw_c:
        c.wait_recv()
    for c in fine_c:
        c.wait_recv()
    own_rows = [lateral_of(1), lateral_of(2)]
    LAT[1] = own_rows[0]
    LAT[2] = own_rows[1]
    same = [o for o in PLANE_OFF if o[2] == 0]
    first_stats = row_stats(own_rows)
    plane1 = send_plane(0, first_stats, same)

    halo_c = [
        remote(X.at[1], X.at[3], s_halo.at[0], r_halo.at[0], above),
        remote(X.at[2], X.at[0], s_halo.at[1], r_halo.at[1], below),
    ]
    for c in halo_c:
        c.start()
    for c in w_c + m_c:
        c.start()
    for c in coarse_c:
        c.wait_recv()
    coarse_halo = [
        remote(C.at[1], C.at[2], s_halo.at[2], r_halo.at[2], above),
        remote(C.at[1], C.at[0], s_halo.at[3], r_halo.at[3], below),
    ]
    for c in coarse_halo:
        c.start()

    for c in plane1:
        c.wait_recv()
    t = first_stats
    for k, o in enumerate(PLANE_OFF):
        if o in same:
            t = t + plane_dst[0, k]
    line_src[0] = jnp.concatenate([t, jnp.zeros((1, 128), f32)], 0)
    line1 = send_line(0)

    for c in par_c:
        c.wait_recv()
    turned = jnp.transpose(jnp.concatenate([PB[...].reshape(64, 128), jnp.zeros((64, 128), f32)], 0))

    def param(j):
        col = jnp.concatenate([turned[0:32, 8 * s + j : 8 * s + j + 1] for s in range(8)], 0)
        return jnp.broadcast_to(col, (D, 128))

    for c in halo_c:
        c.wait_recv()
    LAT[0] = lateral_of(0)
    LAT[3] = lateral_of(3)
    for c in coarse_halo:
        c.wait_recv()
    wide = [jnp.dot(C[s].reshape(256, 256), widen, preferred_element_type=f32) for s in range(3)]
    top = jnp.where(pair == 0, wide[1], wide[0])
    bottom = jnp.where(pair == 127, wide[1], wide[2])
    UPS[0] = 0.75 * top + 0.25 * wide[1]
    UPS[1] = 0.25 * top + 0.75 * wide[1]
    UPS[2] = 0.75 * wide[1] + 0.25 * bottom
    UPS[3] = 0.25 * wide[1] + 0.75 * bottom

    for c in w_c + m_c:
        c.wait_recv()
    core_c = remote(WC.at[:, :, core], WC.at[:, :, core], s_core, r_core, partner)
    core_c.start()

    for c in line1:
        c.wait_recv()
    a, b = scale_shift(line_total(0)[0:1], param(0), param(1))
    a4 = jnp.concatenate([a] * 4, 1)
    b4 = jnp.concatenate([b] * 4, 1)
    lane = lax.broadcasted_iota(jnp.int32, (D, COLS), 1)
    for s in range(4):
        j = LAT[s] * a4 + b4 + UPS[s]
        if s == 0:
            j = jnp.where(pair == 0, 0.0, j)
        if s == 3:
            j = jnp.where(pair == 127, 0.0, j)
        cols = slice(COLS * s, COLS * (s + 1))
        JS[0:256, cols] = jnp.where(lane == 0, 0.0, pltpu.roll(j, 1, 1)).astype(bf16)
        JS[256:512, cols] = j.astype(bf16)
        JS[512:768, cols] = jnp.where(lane == COLS - 1, 0.0, pltpu.roll(j, COLS - 1, 1)).astype(bf16)

    core_c.wait_recv()
    acc = None
    for tap in range(3):
        w = jnp.concatenate([WC[3 * tap + i].reshape(256, 256) for i in range(3)], 1)
        term = jnp.dot(w, JS[:, COLS * tap : COLS * (tap + 2)], preferred_element_type=f32)
        acc = term if acc is None else acc + term
    CO[0] = acc[:, :COLS].astype(bf16)
    CO[1] = acc[:, COLS:].astype(bf16)
    second_stats = row_stats([acc[:, :COLS], acc[:, COLS:]])
    plane2 = send_plane(1, second_stats, PLANE_OFF)
    row_c = remote(CO.at[1 - yl], RC, s_row, r_row, other)
    row_c.start()
    for c in plane2:
        c.wait_recv()
    mine, others = second_stats, None
    for k, o in enumerate(PLANE_OFF):
        v = plane_dst[1, k]
        if o[2] == 0:
            mine = mine + v
        else:
            others = v if others is None else others + v
    line_src[1] = jnp.concatenate([mine, others], 0)
    line2 = send_line(1)
    for c in line2:
        c.wait_recv()
    total = line_total(1)
    gain2, shift2, bias = param(2), param(3), param(4)
    bias4 = jnp.concatenate([bias] * 4, 1)
    mask_w = WC[9].reshape(256, 256)
    row_c.wait_recv()
    for who in range(2):
        a, b = scale_shift(total[who : who + 1], gain2, shift2)
        row = CO[yl] if who == 0 else RC[...]
        act = jnp.maximum(
            row.astype(f32) * jnp.concatenate([a] * 4, 1) + jnp.concatenate([b] * 4, 1), 0.0
        ).astype(bf16)
        feat = (jnp.dot(mask_w, act, preferred_element_type=f32) + bias4).astype(bf16)
        logits = jnp.dot(queries[...], feat, preferred_element_type=f32)
        shifted = logits - jnp.max(logits, 0, keepdims=True)
        res = shifted - jnp.log(jnp.sum(jnp.exp(shifted), 0, keepdims=True))
        out[yl if who == 0 else 1 - yl] = res

    for group in (fine_c, latw_c, par_c, coarse_c, w_c, m_c, halo_c, coarse_halo, plane1, plane2,
                  line1, line2, [core_c, row_c]):
        for c in group:
            c.wait_send()


def per_device(
    fine_features, coarse_level, lat_weight, lat_gain, lat_shift, out_weight, out_gain, out_shift,
    mask_weight, mask_bias, queries,
):
    pixels = float(D // GROUPS * 256 * COLS)
    fine = jnp.transpose(fine_features, (0, 2, 1, 3))
    coarse = jnp.transpose(coarse_level, (0, 2, 1, 3))
    vec = lambda v: v.reshape(1, 32)
    V = pltpu.VMEM
    dma = pltpu.SemaphoreType.DMA
    out = pl.pallas_call(
        functools.partial(kernel, pixels),
        out_shape=jax.ShapeDtypeStruct((2, 200, COLS), f32),
        in_specs=[pl.BlockSpec(memory_space=V)] * 11,
        out_specs=pl.BlockSpec(memory_space=V),
        scratch_shapes=[
            V((4, 8, 24, COLS), bf16),
            V((3, 8, 32, 256), bf16),
            V((8, 32, 192), bf16),
            V((10, 8, 2, 16, 256), bf16),
            V((8, 8, 128), f32),
            V((8, 128), f32),
            V((4, D, COLS), f32),
            V((4, D, COLS), f32),
            V((3 * D, 4 * COLS), bf16),
            V((2, D, COLS), bf16),
            V((D, COLS), bf16),
            V((2, 1, 128), f32),
            V((2, 15, 1, 128), f32),
            V((2, 2, 128), f32),
            V((2, 15, 2, 128), f32),
        ]
        + [dma((7,))] * 12
        + [dma((4,))] * 2
        + [dma] * 2
        + [dma((2, 15))] * 4
        + [dma] * 2,
        compiler_params=pltpu.CompilerParams(
            collective_id=0, has_side_effects=True, vmem_limit_bytes=56 * 1024 * 1024
        ),
        name="merge",
    )(
        fine, coarse, lat_weight, vec(lat_gain), vec(lat_shift),
        out_weight.reshape(9, 2, 16, 256), vec(out_gain), vec(out_shift),
        mask_weight.reshape(2, 16, 256), vec(mask_bias), queries,
    )
    return out.reshape(2, 200, 1, COLS)


def solution(mesh):
    finer = Mesh(mesh.devices.reshape(8, 2, 2, 4, 2), AXES)
    return jax.shard_map(
        per_device,
        mesh=finer,
        in_specs=(
            P(None, CHAN, BAND, None),
            P(None, CHAN, BAND, None),
            P(CHAN, None),
            P(CHAN),
            P(CHAN),
            P(None, None, CHAN, None),
            P(CHAN),
            P(CHAN),
            P(CHAN, None),
            P(CHAN),
            P(),
        ),
        out_specs=P(None, None, AXES, None),
        check_vma=False,
    )
```

time: 196 us -> 59.7 us (0.30)
  blocking collectives: 64.3 us -> 0 us
  waiting for transfers between devices: 56.2 us -> 0 us
  Pallas kernels: 0 us -> 53.1 us
  starting transfers between devices: 26.5 us -> 0 us
  between operations: 13.8 us -> 0.01 us
  matrix products: 11.9 us -> 0 us
  local copies, waits for them, and re-layouts: 17.5 us -> 6.3 us
  other arithmetic: 4.01 us -> 0 us
    pallas_call x0 -> x1, Pallas kernels: none -> 53.1 us  [per_device(): pl.pallas_call(functools.partial(kernel, pixels), out_shape=jax.ShapeDtyp...]
    all_gather x2 -> x0, waiting for transfers between devices: 43.8 us -> none  [the longest x1 31.8 us: whole_of(): shard = lax.all_gather(shard, axis, axis=dim, tiled=True)]
    psum x5 -> x0, blocking collectives: 39.2 us -> none  [over_axes_2(): return functools.reduce(lax.psum, axes, shard)]
    ppermute x4 -> x0, starting transfers between devices: 15.9 us -> none  [the longest x1 7.37 us: extended_2(): lax.ppermute(tail, axis, [(i, (i + 1) % count) for i in range(ends)])]
    all_to_all x1 -> x0, blocking collectives: 14.5 us -> none  [per_device(): lax.all_to_all(joined, CHAN, split_axis=2, concat_axis=1, tiled=True)]
    dot_general x11 -> x0, matrix products: 11.9 us -> none  [the longest x9 7.3 us: conv_taps(): jnp.einsum('oc,ncrw->norw', taps_weight[row_tap, col_tap], window, prefer...]
    all_gather x1 -> x0, blocking collectives: 10.6 us -> none  [whole_of(): shard = lax.all_gather(shard, axis, axis=dim, tiled=True)]
    all_to_all x1 -> x0, starting transfers between devices: 10.5 us -> none  [from_everyone(): lax.all_to_all(jnp.broadcast_to(shard[None], (devices, *shard.shape)), ax...]
  transfers between devices with their start and end apart: 7 -> 0, of which waited for: 6 -> 0; matrix products, arithmetic and copies ran while one was open for 9% -> 0% of each run, Pallas kernels for 0% -> 0%
where the time goes in v1:
time: 59.7 us; the launch traced here: 59.5 us
  Pallas kernels  53.1 us (89%)
  local copies, waits for them, and re-layouts  6.3 us (11%)
    pallas_call x1, Pallas kernels, per_device(): pl.pallas_call(functools.partial(kernel, pixels), out_shape=jax.ShapeDtyp...  53.1 us
    unnamed x2, local copies, waits for them, and re-layouts  3.43 us
    reshape x1, local copies, waits for them, and re-layouts, per_device(): return out.reshape(2, 200, 1, COLS)  2.88 us

profile of v1, /device:TPU:1, one launch (start us, length us, event | category | flops | bytes accessed | tf_op | source)
XLA Modules:
  0.0 59.5 jit_solution(11606020394621372309)
XLA Ops:
  0.0 1.6 %copy.18 = bf16[2,32,4,256]{3,1,2,0:T(8,128)(2,1)} copy(bf16[2,32,4,256]{3,2,1,0:T(4,128)(2,1)} %param.12) | data formatting | bytes 262144 | tf_op args[1]
  1.6 1.9 %copy.17 = bf16[2,24,8,512]{3,1,2,0:T(8,128)(2,1)} copy(bf16[2,24,8,512]{3,2,1,0:T(8,128)(2,1)} %param.11) | data formatting | bytes 786432 | tf_op args[0]
  3.4 53.1 %merge.1 = f32[2,200,512]{2,1,0:T(8,128)} custom-call(bf16[2,8,24,512]{3,2,1,0:T(8,128)(2,1)} %bitcast.15, bf16[2,4,32,256]{3,2,1,0:T(8,128)(2,1)} %bitcast.16, bf16[32,192]{1,0:T(8,128)(2,1)} %latw.1, bf16[1,32]{1,0:T(2,128)(2,1)} %bitcast.19, bf16[1,32]{1,0:T(2,128)(2,1)} %bitcast.20, bf16[9,2,16,256]{3,2,1,0:T(8,128)(2,1)} %bitcast.17, ...), custom_call_target="tpu_custom_call" | custom-call | tf_op jit(solution)/shard_map/merge/pallas_call | solution.py:296
  56.6 2.9 %copy.14 = f32[2,200,1,512]{3,2,1,0:T(1,128)} copy(f32[2,200,1,512]{3,1,0,2:T(8,128)} %bitcast.14) | data formatting | bytes 1638400 | tf_op jit(solution)/shard_map/reshape | solution.py:332

commit v2 on v1

v2 whole, which is shorter than its diff:
```python
import functools

import jax
import jax.numpy as jnp
from jax import lax
from jax.experimental import pallas as pl
from jax.experimental.pallas import tpu as pltpu
from jax.sharding import Mesh
from jax.sharding import PartitionSpec as P

D = 256
GROUPS = 32
COLS = 512
AXES = ("band_0", "band_1", "band_2", "chan_0", "chan_1")
BAND = AXES[:3]
CHAN = AXES[3:]
MESH = pl.DeviceIdType.MESH
f32, bf16 = jnp.float32, jnp.bfloat16
epsilon = 1e-05

CHAN_OFF = [(dx, dy) for dx in (2, 1, 3, 0) for dy in (1, 0) if (dx, dy) != (0, 0)]
PLANE_OFF = [
    (dx, dh, dl)
    for dx in (2, 1, 3, 0)
    for dh in (1, 0)
    for dl in (1, 0)
    if (dx, dh, dl) != (0, 0, 0)
]
SAME_OFF = [o for o in PLANE_OFF if o[2] == 0]
LINE_OFF = [(dz, dc) for dz in (4, 3, 5, 2, 6, 1, 7, 0) for dc in (1, 0) if (dz, dc) != (0, 0)]
DEST = [(xh, dc, dl) for xh in (0, 1) for dc in (0, 1) for dl in (0, 1)]


def kernel(
    pixels,
    fine, coarse, latw, lat_gain, lat_shift, outw, out_gain, out_shift, maskw, mask_bias, queries,
    out,
    FS, FB, CB, WB, X, C, WL, WC, PB, pstage, LAT, UPS, JS, CO, R,
    plane_src, plane_dst, line_src, line_dst,
    s_fine, r_fine, s_coarse, r_coarse, s_latw, r_latw, s_par, r_par, s_w, r_w,
    s_halo, r_halo, s_z, r_z, s_core, r_core, s_plane, r_plane, s_line, r_line, s_row, r_row,
):
    z, yh, core = (lax.axis_index(a) for a in BAND)
    x, yl = (lax.axis_index(a) for a in CHAN)
    me = x * 2 + yl
    pair = (z * 2 + yh) * 8 + x * 2 + core
    half = lax.rem(z, 2)

    def chan_peer(dx, dy, dc=0):
        return (z, yh, lax.rem(core + dc, 2), lax.rem(x + dx, 4), lax.rem(yl + dy, 2))

    def plane_peer(dx, dh, dl):
        return (z, lax.rem(yh + dh, 2), core, lax.rem(x + dx, 4), lax.rem(yl + dl, 2))

    def line_peer(dz, dc):
        return (lax.rem(z + dz, 8), yh, lax.rem(core + dc, 2), x, yl)

    def pair_owner(g):
        k, p = lax.div(g, 8), lax.rem(g, 8)
        return (lax.div(k, 2), lax.rem(k, 2), lax.rem(p, 2), lax.div(p, 2), yl)

    above = pair_owner(lax.rem(pair + 127, 128))
    below = pair_owner(lax.rem(pair + 1, 128))
    partner = (z, yh, 1 - core, x, yl)

    def remote(src, dst, send, recv, dev):
        return pltpu.make_async_remote_copy(
            src_ref=src, dst_ref=dst, send_sem=send, recv_sem=recv,
            device_id=dev, device_id_type=MESH,
        )

    barrier = pltpu.get_barrier_semaphore()
    peers = (
        [plane_peer(*o) for o in PLANE_OFF]
        + [line_peer(*o) for o in LINE_OFF]
        + [chan_peer(*o, 1) for o in CHAN_OFF]
        + [above, below]
    )
    for dev in peers:
        pl.semaphore_signal(barrier, inc=1, device_id=dev, device_id_type=MESH)

    for k in range(4):
        cols = slice(128 * k, 128 * (k + 1))
        FS[384 * k : 384 * (k + 1)] = fine[:, cols].astype(f32)
        for n in range(2):
            for r in range(8):
                FB[n, r, :, cols] = FS[pl.ds(384 * k + 192 * n + r, 24, stride=8), :].astype(bf16)
    for n in range(2):
        rows = coarse[n].astype(f32)
        for r in range(4):
            CB[n, r] = rows[:, r, :].astype(bf16)
    WB[0:9] = outw[...]
    WB[9] = maskw[...]
    pstage[...] = jnp.zeros_like(pstage)
    for j, ref in enumerate((lat_gain, lat_shift, out_gain, out_shift, mask_bias)):
        pstage[j : j + 1, 0:32] = ref[...].astype(f32)
    PB[me] = pstage[...]
    WL[me, core] = latw[core]
    WC[pl.ds(5 * half, 5), me, core] = WB[pl.ds(5 * half, 5), core]
    pl.semaphore_wait(barrier, len(peers))

    latw_c, par_c, w_c = [], [], []
    for k, o in enumerate(CHAN_OFF):
        dev = chan_peer(*o)
        latw_c.append(remote(latw.at[core], WL.at[me, core], s_latw.at[k], r_latw.at[k], dev))
        par_c.append(remote(pstage, PB.at[me], s_par.at[k], r_par.at[k], dev))
        w_c.append(remote(WB.at[pl.ds(5 * half, 5), core], WC.at[pl.ds(5 * half, 5), me, core],
                          s_w.at[k], r_w.at[k], dev))
    for c in latw_c:
        c.start()
    shares = []
    for k, (xh, dc, dl) in enumerate(DEST):
        xd = 2 * core + xh
        dev = (z, yh, dc, xd, dl)
        is_self = (xd == x) & (dc == core) & (dl == yl)
        pos = 2 * xh + dc
        cf = remote(FB.at[dl, pl.ds(2 * pos, 2)], X.at[pl.ds(1, 2), me], s_fine.at[k], r_fine.at[me], dev)
        cc = remote(CB.at[dl, pos], C.at[1, me], s_coarse.at[k], r_coarse.at[me], dev)
        shares.append((is_self, cf, cc))

        @pl.when(is_self)
        def _():
            X[pl.ds(1, 2), me] = FB[dl, pl.ds(2 * pos, 2)]
            C[1, me] = CB[dl, pos]

        @pl.when(jnp.logical_not(is_self))
        def _():
            cf.start()

    for is_self, _, cc in shares:
        @pl.when(jnp.logical_not(is_self))
        def _():
            cc.start()

    for c in w_c:
        c.start()
    for c in par_c:
        c.start()

    def wait_shares(buf, width, send, recv):
        for s in range(8):
            @pl.when(jnp.logical_not((s == me) & (lax.div(x, 2) == core)))
            def _():
                dst = buf.at[pl.ds(1, width), s]
                remote(dst, dst, send.at[s], recv.at[s], partner).wait_recv()

    ci = lax.broadcasted_iota(jnp.int32, (256, COLS), 0)
    cj = lax.broadcasted_iota(jnp.int32, (256, COLS), 1)
    center = lax.shift_right_logical(cj, 1)
    side = jnp.clip(jnp.where(lax.bitwise_and(cj, 1) == 0, center - 1, center + 1), 0, 255)
    widen = (jnp.where(ci == center, 0.75, 0.0) + jnp.where(ci == side, 0.25, 0.0)).astype(bf16)

    def lateral_of(slot):
        rows = X[slot].astype(f32).reshape(192, COLS).astype(bf16)
        return jnp.dot(WL[...].reshape(256, 192), rows, preferred_element_type=f32)

    def row_stats(rows):
        s = q = None
        for row in rows:
            for k in range(COLS // 128):
                t = row[:, 128 * k : 128 * (k + 1)]
                s = t if s is None else s + t
                q = t * t if q is None else q + t * t
        both = jnp.concatenate(
            [jnp.sum(s.reshape(GROUPS, 8, 128), 1), jnp.sum(q.reshape(GROUPS, 8, 128), 1),
             jnp.zeros((64, 128), f32)], 0)
        return jnp.sum(jnp.transpose(both), 0, keepdims=True)

    def scale_shift(total, gain, shift):
        tall = jnp.transpose(jnp.broadcast_to(total, (128, 128)))
        mean = tall[0:32] / pixels
        var = tall[32:64] / pixels - mean * mean
        rstd = lax.rsqrt(var + epsilon)
        spread = lambda v: jnp.broadcast_to(v[:, None, :], (GROUPS, 8, 128)).reshape(D, 128)
        a = spread(rstd) * gain
        return a, shift - spread(mean) * a

    def send_plane(it, offsets):
        done = []
        for k, o in enumerate(PLANE_OFF):
            if o in offsets:
                c = remote(plane_src.at[it], plane_dst.at[it, k], s_plane.at[it, k],
                           r_plane.at[it, k], plane_peer(*o))
                c.start()
                done.append(c)
        return done

    def send_line(it):
        done = []
        for k, o in enumerate(LINE_OFF):
            c = remote(line_src.at[it], line_dst.at[it, k], s_line.at[it, k],
                       r_line.at[it, k], line_peer(*o))
            c.start()
            done.append(c)
        return done

    def line_total(it):
        t = line_src[it]
        for k in range(len(LINE_OFF)):
            t = t + line_dst[it, k]
        return t

    for c in latw_c:
        c.wait_recv()
    latw_core = remote(WL.at[:, core], WL.at[:, core], s_core.at[0], r_core.at[0], partner)
    latw_core.start()
    wait_shares(X, 2, s_fine, r_fine)
    latw_core.wait_recv()
    own_rows = [lateral_of(1), lateral_of(2)]
    LAT[1] = own_rows[0]
    LAT[2] = own_rows[1]
    line_src[0] = jnp.concatenate([row_stats(own_rows), jnp.zeros((1, 128), f32)], 0)
    line1 = send_line(0)

    halo_c = [
        remote(X.at[1], X.at[3], s_halo.at[0], r_halo.at[0], above),
        remote(X.at[2], X.at[0], s_halo.at[1], r_halo.at[1], below),
    ]
    for c in halo_c:
        c.start()
    wait_shares(C, 1, s_coarse, r_coarse)
    coarse_halo = [
        remote(C.at[1], C.at[2], s_halo.at[2], r_halo.at[2], above),
        remote(C.at[1], C.at[0], s_halo.at[3], r_halo.at[3], below),
    ]
    for c in coarse_halo:
        c.start()

    for c in line1:
        c.wait_recv()
    plane_src[0] = line_total(0)[0:1]
    plane1 = send_plane(0, SAME_OFF)

    for c in w_c:
        c.wait_recv()
    mine = pl.ds(5 * half, 5)
    yours = pl.ds(5 * (1 - half), 5)
    lower = WC.at[mine, pl.ds(0, 4), core]
    upper = WC.at[mine, pl.ds(4, 4), core]
    z_c = [
        remote(lower, lower, s_z.at[0], r_z.at[0], line_peer(1, 0)),
        remote(upper, upper, s_z.at[1], r_z.at[1], line_peer(7, 0)),
    ]
    for c in z_c:
        c.start()
    core_c = [remote(WC.at[mine, :, core], WC.at[mine, :, core], s_core.at[1], r_core.at[1], partner)]
    core_c[0].start()

    for c in par_c:
        c.wait_recv()
    turned = jnp.transpose(jnp.concatenate([PB[...].reshape(64, 128), jnp.zeros((64, 128), f32)], 0))

    def param(j):
        col = jnp.concatenate([turned[0:32, 8 * s + j : 8 * s + j + 1] for s in range(8)], 0)
        return jnp.broadcast_to(col, (D, 128))

    for c in halo_c:
        c.wait_recv()
    LAT[0] = lateral_of(0)
    LAT[3] = lateral_of(3)
    for c in coarse_halo:
        c.wait_recv()
    wide = [jnp.dot(C[s].reshape(256, 256), widen, preferred_element_type=f32) for s in range(3)]
    top = jnp.where(pair == 0, wide[1], wide[0])
    bottom = jnp.where(pair == 127, wide[1], wide[2])
    UPS[0] = 0.75 * top + 0.25 * wide[1]
    UPS[1] = 0.25 * top + 0.75 * wide[1]
    UPS[2] = 0.75 * wide[1] + 0.25 * bottom
    UPS[3] = 0.25 * wide[1] + 0.75 * bottom

    your_lower = WC.at[yours, pl.ds(0, 4), core]
    your_upper = WC.at[yours, pl.ds(4, 4), core]
    remote(your_lower, your_lower, s_z.at[0], r_z.at[0], partner).wait_recv()
    remote(your_upper, your_upper, s_z.at[1], r_z.at[1], partner).wait_recv()
    core_c.append(
        remote(WC.at[yours, :, core], WC.at[yours, :, core], s_core.at[2], r_core.at[2], partner)
    )
    core_c[1].start()

    for c in plane1:
        c.wait_recv()
    t = plane_src[0]
    for k, o in enumerate(PLANE_OFF):
        if o in SAME_OFF:
            t = t + plane_dst[0, k]
    a, b = scale_shift(t, param(0), param(1))
    a4 = jnp.concatenate([a] * 4, 1)
    b4 = jnp.concatenate([b] * 4, 1)
    lane = lax.broadcasted_iota(jnp.int32, (D, COLS), 1)
    for s in range(4):
        j = LAT[s] * a4 + b4 + UPS[s]
        if s == 0:
            j = jnp.where(pair == 0, 0.0, j)
        if s == 3:
            j = jnp.where(pair == 127, 0.0, j)
        cols = slice(COLS * s, COLS * (s + 1))
        JS[0:256, cols] = jnp.where(lane == 0, 0.0, pltpu.roll(j, 1, 1)).astype(bf16)
        JS[256:512, cols] = j.astype(bf16)
        JS[512:768, cols] = jnp.where(lane == COLS - 1, 0.0, pltpu.roll(j, COLS - 1, 1)).astype(bf16)

    for part, c in ((mine, core_c[0]), (yours, core_c[1])):
        from_partner = WC.at[part, :, 1 - core]
        remote(from_partner, from_partner, s_core.at[1], r_core.at[1 if c is core_c[0] else 2],
               partner).wait_recv()
    acc = None
    for tap in range(3):
        w = jnp.concatenate([WC[3 * tap + i].reshape(256, 256) for i in range(3)], 1)
        term = jnp.dot(w, JS[:, COLS * tap : COLS * (tap + 2)], preferred_element_type=f32)
        acc = term if acc is None else acc + term
    CO[0] = acc[:, :COLS].astype(bf16)
    CO[1] = acc[:, COLS:].astype(bf16)
    plane_src[1] = row_stats([acc[:, :COLS], acc[:, COLS:]])
    plane2 = send_plane(1, PLANE_OFF)
    xf = lax.rem(2 * x + core, 4)
    kept = (xf == x) & (lax.div(x, 2) == core)
    row_c = []
    for j in range(2):
        is_self = kept & (yl == j)
        c = remote(CO.at[j], R.at[yl], s_row.at[j], r_row.at[yl], (z, yh, lax.div(x, 2), xf, j))
        row_c.append((is_self, c))

        @pl.when(is_self)
        def _():
            R[yl] = CO[j]

        @pl.when(jnp.logical_not(is_self))
        def _():
            c.start()

    for c in plane2:
        c.wait_recv()
    mine_sum, other_sum = plane_src[1], None
    for k, o in enumerate(PLANE_OFF):
        v = plane_dst[1, k]
        if o[2] == 0:
            mine_sum = mine_sum + v
        else:
            other_sum = v if other_sum is None else other_sum + v
    line_src[1] = jnp.concatenate([mine_sum, other_sum], 0)
    line2 = send_line(1)
    gain2, shift2, bias = param(2), param(3), param(4)
    bias4 = jnp.concatenate([bias] * 4, 1)
    for n in range(2):
        @pl.when(jnp.logical_not(kept & (yl == n)))
        def _():
            remote(R.at[n], R.at[n], s_row.at[n], r_row.at[n], partner).wait_recv()

    for c in line2:
        c.wait_recv()
    total = line_total(1)
    mask_w = WC[9].reshape(256, 256)
    for who in range(2):
        image = yl if who == 0 else 1 - yl
        a, b = scale_shift(total[who : who + 1], gain2, shift2)
        act = jnp.maximum(
            R[image].astype(f32) * jnp.concatenate([a] * 4, 1) + jnp.concatenate([b] * 4, 1), 0.0
        ).astype(bf16)
        feat = (jnp.dot(mask_w, act, preferred_element_type=f32) + bias4).astype(bf16)
        logits = jnp.dot(queries[...], feat, preferred_element_type=f32)
        shifted = logits - jnp.max(logits, 0, keepdims=True)
        res = shifted - jnp.log(jnp.sum(jnp.exp(shifted), 0, keepdims=True))
        for k in range(4):
            out[image, pl.ds(k, 200, stride=4), :] = res[:, 128 * k : 128 * (k + 1)]

    for group in (latw_c, par_c, w_c, [latw_core], halo_c, coarse_halo, z_c, core_c, plane1, plane2,
                  line1, line2):
        for c in group:
            c.wait_send()
    for is_self, *cs in shares + row_c:
        @pl.when(jnp.logical_not(is_self))
        def _():
            for c in cs:
                c.wait_send()


def per_device(
    fine_features, coarse_level, lat_weight, lat_gain, lat_shift, out_weight, out_gain, out_shift,
    mask_weight, mask_bias, queries,
):
    pixels = float(D // GROUPS * 256 * COLS)
    vec = lambda v: v.reshape(1, 32)
    V = pltpu.VMEM
    dma = pltpu.SemaphoreType.DMA
    out = pl.pallas_call(
        functools.partial(kernel, pixels),
        out_shape=jax.ShapeDtypeStruct((2, 800, 128), f32),
        in_specs=[pl.BlockSpec(memory_space=V)] * 11,
        out_specs=pl.BlockSpec(memory_space=V),
        scratch_shapes=[
            V((4 * 384, 128), f32),
            V((2, 8, 24, COLS), bf16),
            V((2, 4, 32, 256), bf16),
            V((10, 2, 16, 256), bf16),
            V((4, 8, 24, COLS), bf16),
            V((3, 8, 32, 256), bf16),
            V((8, 2, 16, 192), bf16),
            V((10, 8, 2, 16, 256), bf16),
            V((8, 8, 128), f32),
            V((8, 128), f32),
            V((4, D, COLS), f32),
            V((4, D, COLS), f32),
            V((3 * D, 4 * COLS), bf16),
            V((2, D, COLS), bf16),
            V((2, D, COLS), bf16),
            V((2, 1, 128), f32),
            V((2, 15, 1, 128), f32),
            V((2, 2, 128), f32),
            V((2, 15, 2, 128), f32),
        ]
        + [dma((8,))] * 4
        + [dma((7,))] * 6
        + [dma((4,))] * 2
        + [dma((2,))] * 2
        + [dma((3,))] * 2
        + [dma((2, 15))] * 4
        + [dma((2,))] * 2,
        compiler_params=pltpu.CompilerParams(
            collective_id=0, has_side_effects=True, vmem_limit_bytes=56 * 1024 * 1024
        ),
        name="merge",
    )(
        fine_features.reshape(384, COLS), coarse_level, lat_weight.reshape(2, 16, 192),
        vec(lat_gain), vec(lat_shift),
        out_weight.reshape(9, 2, 16, 256), vec(out_gain), vec(out_shift),
        mask_weight.reshape(2, 16, 256), vec(mask_bias), queries,
    )
    return out.reshape(2, 200, 1, COLS)


def solution(mesh):
    finer = Mesh(mesh.devices.reshape(8, 2, 2, 4, 2), AXES)
    return jax.shard_map(
        per_device,
        mesh=finer,
        in_specs=(
            P(None, CHAN, BAND, None),
            P(None, CHAN, BAND, None),
            P(CHAN, None),
            P(CHAN),
            P(CHAN),
            P(None, None, CHAN, None),
            P(CHAN),
            P(CHAN),
            P(CHAN, None),
            P(CHAN),
            P(),
        ),
        out_specs=P(None, None, AXES, None),
        check_vma=False,
    )
```

time: 59.7 us -> 52.6 us (0.88)
  local copies, waits for them, and re-layouts: 6.3 us -> 2.6 us
  Pallas kernels: 53.1 us -> 49.8 us
    pallas_call x1, Pallas kernels: 53.1 us -> 49.8 us  [per_device(): pl.pallas_call(functools.partial(kernel, pixels), out_shape=jax.ShapeDtyp...]
    reshape x1 -> x0, local copies, waits for them, and re-layouts: 2.88 us -> none  [per_device(): return out.reshape(2, 200, 1, COLS)]
    unnamed x2 -> x1, local copies, waits for them, and re-layouts: 3.43 us -> 2.6 us
where the time goes in v2:
time: 52.6 us; the launch traced here: 52.4 us
  Pallas kernels  49.8 us (95%)
  local copies, waits for them, and re-layouts  2.6 us (5%)
    pallas_call x1, Pallas kernels, per_device(): pl.pallas_call(functools.partial(kernel, pixels), out_shape=jax.ShapeDtyp...  49.8 us
    unnamed x1, local copies, waits for them, and re-layouts  2.6 us

profile of v2, /device:TPU:1, one launch (start us, length us, event | category | flops | bytes accessed | tf_op | source)
XLA Modules:
  0.0 52.4 jit_solution(12267003695852543591)
XLA Ops:
  0.0 49.8 %merge.1 = f32[2,800,128]{2,1,0:T(8,128)} custom-call(bf16[384,512]{1,0:T(8,128)(2,1)} %bitcast.11, bf16[2,32,4,256]{3,2,1,0:T(4,128)(2,1)} %coarse.1, bf16[2,16,192]{2,1,0:T(8,128)(2,1)} %bitcast.13, bf16[1,32]{1,0:T(2,128)(2,1)} %bitcast.15, bf16[1,32]{1,0:T(2,128)(2,1)} %bitcast.16, bf16[9,2,16,256]{3,2,1,0:T(8,128)(2,1)} %bitcast.12, ...), custom_call_target="tpu_custom_call" | custom-call | tf_op jit(solution)/shard_map/merge/pallas_call | solution.py:384
  49.8 2.6 %copy.14 = f32[2,200,1,512]{3,2,1,0:T(1,128)} copy(f32[2,200,1,512]{3,2,1,0:T(1,128)} %bitcast.10) | data formatting | bytes 1638400

commit v3 on v2

--- a/solution.py
+++ b/solution.py
@@ -26,15 +26,16 @@
     for dl in (1, 0)
     if (dx, dh, dl) != (0, 0, 0)
 ]
-SAME_OFF = [o for o in PLANE_OFF if o[2] == 0]
+SAME_OFF = [o for o in PLANE_OFF if o[1] == o[2]]
 LINE_OFF = [(dz, dc) for dz in (4, 3, 5, 2, 6, 1, 7, 0) for dc in (1, 0) if (dz, dc) != (0, 0)]
-DEST = [(xh, dc, dl) for xh in (0, 1) for dc in (0, 1) for dl in (0, 1)]
+DEST = [(0, 0, 1), (1, 1, 0), (0, 0, 0), (1, 1, 1), (0, 1, 1), (1, 0, 0), (0, 1, 0), (1, 0, 1)]
 
 
 def kernel(
     pixels,
-    fine, coarse, latw, lat_gain, lat_shift, outw, out_gain, out_shift, maskw, mask_bias, queries,
-    out,
+    fine_in, coarse_in, latw_in, lat_gain, lat_shift, outw_in, out_gain, out_shift, maskw_in, mask_bias,
+    act_out, mask_out, bias_out,
+    fine, coarse, latw, PV, s_in,
     FS, FB, CB, WB, X, C, WL, WC, PB, pstage, LAT, UPS, JS, CO, R,
     plane_src, plane_dst, line_src, line_dst,
     s_fine, r_fine, s_coarse, r_coarse, s_latw, r_latw, s_par, r_par, s_w, r_w,
@@ -43,7 +44,10 @@
     z, yh, core = (lax.axis_index(a) for a in BAND)
     x, yl = (lax.axis_index(a) for a in CHAN)
     me = x * 2 + yl
-    pair = (z * 2 + yh) * 8 + x * 2 + core
+    fold = lambda v, odd: v + odd * (3 - 2 * v)
+    xe = fold(x, yh)
+    img = lax.rem(yl + yh, 2)
+    pair = (z * 2 + yh) * 8 + xe * 2 + core
     half = lax.rem(z, 2)
 
     def chan_peer(dx, dy, dc=0):
@@ -57,7 +61,8 @@
 
     def pair_owner(g):
         k, p = lax.div(g, 8), lax.rem(g, 8)
-        return (lax.div(k, 2), lax.rem(k, 2), lax.rem(p, 2), lax.div(p, 2), yl)
+        odd = lax.rem(k, 2)
+        return (lax.div(k, 2), odd, lax.rem(p, 2), fold(lax.div(p, 2), odd), lax.rem(img + odd, 2))
 
     above = pair_owner(lax.rem(pair + 127, 128))
     below = pair_owner(lax.rem(pair + 1, 128))
@@ -79,21 +84,32 @@
     for dev in peers:
         pl.semaphore_signal(barrier, inc=1, device_id=dev, device_id_type=MESH)
 
+    loads = [
+        pltpu.make_async_copy(src, dst, s_in.at[i])
+        for i, (src, dst) in enumerate(
+            [(fine_in, fine), (latw_in, latw), (coarse_in, coarse), (outw_in, WB.at[pl.ds(0, 9)]),
+             (maskw_in, WB.at[9])]
+            + [(v, PV.at[j]) for j, v in enumerate((lat_gain, lat_shift, out_gain, out_shift, mask_bias))]
+        )
+    ]
+    for c in loads:
+        c.start()
+    loads[0].wait()
     for k in range(4):
         cols = slice(128 * k, 128 * (k + 1))
         FS[384 * k : 384 * (k + 1)] = fine[:, cols].astype(f32)
         for n in range(2):
             for r in range(8):
                 FB[n, r, :, cols] = FS[pl.ds(384 * k + 192 * n + r, 24, stride=8), :].astype(bf16)
+    for c in loads[1:]:
+        c.wait()
     for n in range(2):
         rows = coarse[n].astype(f32)
         for r in range(4):
             CB[n, r] = rows[:, r, :].astype(bf16)
-    WB[0:9] = outw[...]
-    WB[9] = maskw[...]
     pstage[...] = jnp.zeros_like(pstage)
-    for j, ref in enumerate((lat_gain, lat_shift, out_gain, out_shift, mask_bias)):
-        pstage[j : j + 1, 0:32] = ref[...].astype(f32)
+    for j in range(5):
+        pstage[j : j + 1, 0:32] = PV[j].astype(f32)
     PB[me] = pstage[...]
     WL[me, core] = latw[core]
     WC[pl.ds(5 * half, 5), me, core] = WB[pl.ds(5 * half, 5), core]
@@ -109,19 +125,21 @@
     for c in latw_c:
         c.start()
     shares = []
-    for k, (xh, dc, dl) in enumerate(DEST):
-        xd = 2 * core + xh
+    for k, (ax, ac, al) in enumerate(DEST):
+        xh, dc, dl = lax.rem(x + ax, 2), lax.rem(yl + ac, 2), lax.rem(yl + al, 2)
+        xd = fold(2 * core + xh, yh)
+        image = lax.rem(dl + yh, 2)
         dev = (z, yh, dc, xd, dl)
         is_self = (xd == x) & (dc == core) & (dl == yl)
         pos = 2 * xh + dc
-        cf = remote(FB.at[dl, pl.ds(2 * pos, 2)], X.at[pl.ds(1, 2), me], s_fine.at[k], r_fine.at[me], dev)
-        cc = remote(CB.at[dl, pos], C.at[1, me], s_coarse.at[k], r_coarse.at[me], dev)
+        cf = remote(FB.at[image, pl.ds(2 * pos, 2)], X.at[pl.ds(1, 2), me], s_fine.at[k], r_fine.at[me], dev)
+        cc = remote(CB.at[image, pos], C.at[1, me], s_coarse.at[k], r_coarse.at[me], dev)
         shares.append((is_self, cf, cc))
 
         @pl.when(is_self)
         def _():
-            X[pl.ds(1, 2), me] = FB[dl, pl.ds(2 * pos, 2)]
-            C[1, me] = CB[dl, pos]
+            X[pl.ds(1, 2), me] = FB[image, pl.ds(2 * pos, 2)]
+            C[1, me] = CB[image, pos]
 
         @pl.when(jnp.logical_not(is_self))
         def _():
@@ -139,7 +157,7 @@
 
     def wait_shares(buf, width, send, recv):
         for s in range(8):
-            @pl.when(jnp.logical_not((s == me) & (lax.div(x, 2) == core)))
+            @pl.when(jnp.logical_not((s == me) & (lax.div(xe, 2) == core)))
             def _():
                 dst = buf.at[pl.ds(1, width), s]
                 remote(dst, dst, send.at[s], recv.at[s], partner).wait_recv()
@@ -209,7 +227,7 @@
     own_rows = [lateral_of(1), lateral_of(2)]
     LAT[1] = own_rows[0]
     LAT[2] = own_rows[1]
-    line_src[0] = jnp.concatenate([row_stats(own_rows), jnp.zeros((1, 128), f32)], 0)
+    line_src[0] = row_stats(own_rows)
     line1 = send_line(0)
 
     halo_c = [
@@ -225,11 +243,6 @@
     ]
     for c in coarse_halo:
         c.start()
-
-    for c in line1:
-        c.wait_recv()
-    plane_src[0] = line_total(0)[0:1]
-    plane1 = send_plane(0, SAME_OFF)
 
     for c in w_c:
         c.wait_recv()
@@ -245,6 +258,11 @@
         c.start()
     core_c = [remote(WC.at[mine, :, core], WC.at[mine, :, core], s_core.at[1], r_core.at[1], partner)]
     core_c[0].start()
+
+    for c in line1:
+        c.wait_recv()
+    plane_src[0] = line_total(0)
+    plane1 = send_plane(0, SAME_OFF)
 
     for c in par_c:
         c.wait_recv()
@@ -309,59 +327,50 @@
         acc = term if acc is None else acc + term
     CO[0] = acc[:, :COLS].astype(bf16)
     CO[1] = acc[:, COLS:].astype(bf16)
-    plane_src[1] = row_stats([acc[:, :COLS], acc[:, COLS:]])
-    plane2 = send_plane(1, PLANE_OFF)
-    xf = lax.rem(2 * x + core, 4)
-    kept = (xf == x) & (lax.div(x, 2) == core)
+    line_src[1] = row_stats([acc[:, :COLS], acc[:, COLS:]])
+    line2 = send_line(1)
+    xf = lax.rem(2 * xe + core, 4)
+    kept = (xf == x) & (lax.div(xe, 2) == core)
     row_c = []
     for j in range(2):
         is_self = kept & (yl == j)
-        c = remote(CO.at[j], R.at[yl], s_row.at[j], r_row.at[yl], (z, yh, lax.div(x, 2), xf, j))
+        c = remote(CO.at[j], R.at[img], s_row.at[j], r_row.at[img], (z, yh, lax.div(xe, 2), xf, j))
         row_c.append((is_self, c))
 
         @pl.when(is_self)
         def _():
-            R[yl] = CO[j]
+            R[img] = CO[j]
 
         @pl.when(jnp.logical_not(is_self))
         def _():
             c.start()
+
+    gain2, shift2, bias = param(2), param(3), param(4)
+    bias_out[...] = bias
+    mask_out[...] = WC[9].reshape(256, 256)
+    for c in line2:
+        c.wait_recv()
+    plane_src[1] = line_total(1)
+    plane2 = send_plane(1, PLANE_OFF)
+    for n in range(2):
+        @pl.when(jnp.logical_not(kept & (img == n)))
+        def _():
+            remote(R.at[n], R.at[n], s_row.at[n], r_row.at[n], partner).wait_recv()
 
     for c in plane2:
         c.wait_recv()
     mine_sum, other_sum = plane_src[1], None
     for k, o in enumerate(PLANE_OFF):
         v = plane_dst[1, k]
-        if o[2] == 0:
+        if o in SAME_OFF:
             mine_sum = mine_sum + v
         else:
             other_sum = v if other_sum is None else other_sum + v
-    line_src[1] = jnp.concatenate([mine_sum, other_sum], 0)
-    line2 = send_line(1)
-    gain2, shift2, bias = param(2), param(3), param(4)
-    bias4 = jnp.concatenate([bias] * 4, 1)
-    for n in range(2):
-        @pl.when(jnp.logical_not(kept & (yl == n)))
-        def _():
-            remote(R.at[n], R.at[n], s_row.at[n], r_row.at[n], partner).wait_recv()
-
-    for c in line2:
-        c.wait_recv()
-    total = line_total(1)
-    mask_w = WC[9].reshape(256, 256)
-    for who in range(2):
-        image = yl if who == 0 else 1 - yl
-        a, b = scale_shift(total[who : who + 1], gain2, shift2)
-        act = jnp.maximum(
+    for image, total in ((img, mine_sum), (1 - img, other_sum)):
+        a, b = scale_shift(total, gain2, shift2)
+        act_out[image] = jnp.maximum(
             R[image].astype(f32) * jnp.concatenate([a] * 4, 1) + jnp.concatenate([b] * 4, 1), 0.0
         ).astype(bf16)
-        feat = (jnp.dot(mask_w, act, preferred_element_type=f32) + bias4).astype(bf16)
-        logits = jnp.dot(queries[...], feat, preferred_element_type=f32)
-        shifted = logits - jnp.max(logits, 0, keepdims=True)
-        res = shifted - jnp.log(jnp.sum(jnp.exp(shifted), 0, keepdims=True))
-        for k in range(4):
-            out[image, pl.ds(k, 200, stride=4), :] = res[:, 128 * k : 128 * (k + 1)]
-
     for group in (latw_c, par_c, w_c, [latw_core], halo_c, coarse_halo, z_c, core_c, plane1, plane2,
                   line1, line2):
         for c in group:
@@ -371,6 +380,16 @@
         def _():
             for c in cs:
                 c.wait_send()
+
+
+def log_probs_of(act, mask_w, bias, queries, out):
+    bias4 = jnp.concatenate([bias[...]] * 4, 1)
+    feat = (jnp.dot(mask_w[...], act[0], preferred_element_type=f32) + bias4).astype(bf16)
+    logits = jnp.dot(queries[...], feat, preferred_element_type=f32)
+    shifted = logits - jnp.max(logits, 0, keepdims=True)
+    res = shifted - jnp.log(jnp.sum(jnp.exp(shifted), 0, keepdims=True))
+    for k in range(4):
+        out[0, pl.ds(k, 200, stride=4), :] = res[:, 128 * k : 128 * (k + 1)]
 
 
 def per_device(
@@ -381,12 +400,22 @@
     vec = lambda v: v.reshape(1, 32)
     V = pltpu.VMEM
     dma = pltpu.SemaphoreType.DMA
-    out = pl.pallas_call(
+    hbm = lambda v: pltpu.with_memory_space_constraint(v, pltpu.HBM)
+    act, mask_w, bias = pl.pallas_call(
         functools.partial(kernel, pixels),
-        out_shape=jax.ShapeDtypeStruct((2, 800, 128), f32),
-        in_specs=[pl.BlockSpec(memory_space=V)] * 11,
-        out_specs=pl.BlockSpec(memory_space=V),
+        out_shape=(
+            jax.ShapeDtypeStruct((2, D, COLS), bf16),
+            jax.ShapeDtypeStruct((D, D), bf16),
+            jax.ShapeDtypeStruct((D, 128), f32),
+        ),
+        in_specs=[pl.BlockSpec(memory_space=pltpu.HBM)] * 10,
+        out_specs=(pl.BlockSpec(memory_space=V),) * 3,
         scratch_shapes=[
+            V((384, COLS), bf16),
+            V((2, 32, 4, 256), bf16),
+            V((2, 16, 192), bf16),
+            V((5, 1, 32), bf16),
+            dma((10,)),
             V((4 * 384, 128), f32),
             V((2, 8, 24, COLS), bf16),
             V((2, 4, 32, 256), bf16),
@@ -404,8 +433,8 @@
             V((2, D, COLS), bf16),
             V((2, 1, 128), f32),
             V((2, 15, 1, 128), f32),
-            V((2, 2, 128), f32),
-            V((2, 15, 2, 128), f32),
+            V((2, 1, 128), f32),
+            V((2, 15, 1, 128), f32),
         ]
         + [dma((8,))] * 4
         + [dma((7,))] * 6
@@ -415,15 +444,29 @@
         + [dma((2, 15))] * 4
         + [dma((2,))] * 2,
         compiler_params=pltpu.CompilerParams(
-            collective_id=0, has_side_effects=True, vmem_limit_bytes=56 * 1024 * 1024
+            collective_id=0, has_side_effects=True, vmem_limit_bytes=40 * 1024 * 1024
         ),
         name="merge",
-    )(
+    )(*map(hbm, (
         fine_features.reshape(384, COLS), coarse_level, lat_weight.reshape(2, 16, 192),
         vec(lat_gain), vec(lat_shift),
         out_weight.reshape(9, 2, 16, 256), vec(out_gain), vec(out_shift),
-        mask_weight.reshape(2, 16, 256), vec(mask_bias), queries,
-    )
+        mask_weight.reshape(2, 16, 256), vec(mask_bias),
+    )))
+    out = pl.pallas_call(
+        log_probs_of,
+        out_shape=jax.ShapeDtypeStruct((2, 800, 128), f32),
+        grid=(2,),
+        in_specs=[
+            pl.BlockSpec((1, D, COLS), lambda n: (n, 0, 0)),
+            pl.BlockSpec((D, D), lambda n: (0, 0)),
+            pl.BlockSpec((D, 128), lambda n: (0, 0)),
+            pl.BlockSpec((200, D), lambda n: (0, 0)),
+        ],
+        out_specs=pl.BlockSpec((1, 800, 128), lambda n: (n, 0, 0)),
+        compiler_params=pltpu.CompilerParams(vmem_limit_bytes=16 * 1024 * 1024),
+        name="log_probs",
+    )(act, mask_w, bias, queries)
     return out.reshape(2, 200, 1, COLS)
 
 

time: 52.6 us -> 47.3 us (0.90); the launches traced: 52.4 us -> 46.4 us
  Pallas kernels: 49.8 us -> 46.4 us
  local copies, waits for them, and re-layouts: 2.6 us -> 0.01 us
    pallas_call x1 -> x2, Pallas kernels: 49.8 us -> 46.4 us  [the longest x1 44.5 us: per_device(): pl.pallas_call(functools.partial(kernel, pixels), out_shape=(jax.ShapeDty...]
    unnamed x1 -> x2, local copies, waits for them, and re-layouts: 2.6 us -> 0.01 us
where the time goes in v3:
time: 47.3 us; the launch traced here: 46.4 us
  Pallas kernels  46.4 us (98%)
    pallas_call x1, Pallas kernels, per_device(): pl.pallas_call(functools.partial(kernel, pixels), out_shape=(jax.ShapeDty...  44.5 us
    pallas_call x1, Pallas kernels, per_device(): pl.pallas_call(log_probs_of, out_shape=jax.ShapeDtypeStruct((2, 800, 128)...  1.87 us

profile of v3, /device:TPU:1, one launch (start us, length us, event | category | flops | bytes accessed | tf_op | source)
XLA Modules:
  0.0 46.4 jit_solution(2454579154078317650)
XLA Ops:
  0.0 0.0 copy-start
  0.0 44.5 %merge.1 = (bf16[2,256,512]{2,1,0:T(8,128)(2,1)S(1)}, bf16[256,256]{1,0:T(8,128)(2,1)S(1)}, f32[256,128]{1,0:T(8,128)S(1)}) custom-call(bf16[384,512]{1,0:T(8,128)(2,1)} %bitcast.10, bf16[2,32,4,256]{3,2,1,0:T(4,128)(2,1)} %coarse_in.1, bf16[2,16,192]{2,1,0:T(8,128)(2,1)} %bitcast.12, bf16[1,32]{1,0:T(2,128)(2,1)} %bitcast.14, bf16[1,32]{1,0:T(2,128)(2,1)} %bitcast.15, ...), custom_call_target="tpu_custom_call" | custom-call | tf_op jit(solution)/shard_map/merge/pallas_call | solution.py:404
  44.5 0.0 copy-done
  44.6 1.9 %log_probs.1 = f32[2,800,128]{2,1,0:T(8,128)} custom-call(bf16[2,256,512]{2,1,0:T(8,128)(2,1)S(1)} %get-tuple-element.8.act, bf16[256,256]{1,0:T(8,128)(2,1)S(1)} %get-tuple-element.9.mask_w, f32[256,128]{1,0:T(8,128)S(1)} %get-tuple-element.10.bias, bf16[200,256]{1,0:T(8,128)(2,1)S(1)} %copy-done), custom_call_target="tpu_custom_call" | custom-call | tf_op jit(solution)/shard_map/log_probs/pallas_call | solution.py:456
Async XLA Ops:
  0.0 44.5 %copy-start = (bf16[200,256]{1,0:T(8,128)(2,1)S(1)}, bf16[200,256]{1,0:T(8,128)(2,1)}, u32[]{:S(2)}) copy-start(bf16[200,256]{1,0:T(8,128)(2,1)} %queries.1) | copy-start | bytes 307204

commit v4 on v3

--- a/solution.py
+++ b/solution.py
@@ -37,7 +37,7 @@
     act_out, mask_out, bias_out,
     fine, coarse, latw, PV, s_in,
     FS, FB, CB, WB, X, C, WL, WC, PB, pstage, LAT, UPS, JS, CO, R,
-    plane_src, plane_dst, line_src, line_dst,
+    plane_src, plane_dst, line_src, line_dst, line_src2, line_dst2,
     s_fine, r_fine, s_coarse, r_coarse, s_latw, r_latw, s_par, r_par, s_w, r_w,
     s_halo, r_halo, s_z, r_z, s_core, r_core, s_plane, r_plane, s_line, r_line, s_row, r_row,
 ):
@@ -101,18 +101,8 @@
         for n in range(2):
             for r in range(8):
                 FB[n, r, :, cols] = FS[pl.ds(384 * k + 192 * n + r, 24, stride=8), :].astype(bf16)
-    for c in loads[1:]:
-        c.wait()
-    for n in range(2):
-        rows = coarse[n].astype(f32)
-        for r in range(4):
-            CB[n, r] = rows[:, r, :].astype(bf16)
-    pstage[...] = jnp.zeros_like(pstage)
-    for j in range(5):
-        pstage[j : j + 1, 0:32] = PV[j].astype(f32)
-    PB[me] = pstage[...]
+    loads[1].wait()
     WL[me, core] = latw[core]
-    WC[pl.ds(5 * half, 5), me, core] = WB[pl.ds(5 * half, 5), core]
     pl.semaphore_wait(barrier, len(peers))
 
     latw_c, par_c, w_c = [], [], []
@@ -134,18 +124,32 @@
         pos = 2 * xh + dc
         cf = remote(FB.at[image, pl.ds(2 * pos, 2)], X.at[pl.ds(1, 2), me], s_fine.at[k], r_fine.at[me], dev)
         cc = remote(CB.at[image, pos], C.at[1, me], s_coarse.at[k], r_coarse.at[me], dev)
-        shares.append((is_self, cf, cc))
+        shares.append((is_self, cf, cc, image, pos))
 
         @pl.when(is_self)
         def _():
             X[pl.ds(1, 2), me] = FB[image, pl.ds(2 * pos, 2)]
-            C[1, me] = CB[image, pos]
 
         @pl.when(jnp.logical_not(is_self))
         def _():
             cf.start()
 
-    for is_self, _, cc in shares:
+    for c in loads[2:]:
+        c.wait()
+    for n in range(2):
+        rows = coarse[n].astype(f32)
+        for r in range(4):
+            CB[n, r] = rows[:, r, :].astype(bf16)
+    pstage[...] = jnp.zeros_like(pstage)
+    for j in range(5):
+        pstage[j : j + 1, 0:32] = PV[j].astype(f32)
+    PB[me] = pstage[...]
+    WC[pl.ds(5 * half, 5), me, core] = WB[pl.ds(5 * half, 5), core]
+    for is_self, _, cc, image, pos in shares:
+        @pl.when(is_self)
+        def _():
+            C[1, me] = CB[image, pos]
+
         @pl.when(jnp.logical_not(is_self))
         def _():
             cc.start()
@@ -248,12 +252,18 @@
         c.wait_recv()
     mine = pl.ds(5 * half, 5)
     yours = pl.ds(5 * (1 - half), 5)
-    lower = WC.at[mine, pl.ds(0, 4), core]
-    upper = WC.at[mine, pl.ds(4, 4), core]
-    z_c = [
-        remote(lower, lower, s_z.at[0], r_z.at[0], line_peer(1, 0)),
-        remote(upper, upper, s_z.at[1], r_z.at[1], line_peer(7, 0)),
-    ]
+    z_c = []
+    for i in range(4):
+        if i == 0:
+            dz = 1
+        elif i == 1:
+            dz = jnp.where((x == 0) & (yh == 1), 7, 1)
+        elif i == 2:
+            dz = jnp.where((x == 0) & (yh == 0), 1, 7)
+        else:
+            dz = 7
+        piece = WC.at[mine, pl.ds(2 * i, 2), core]
+        z_c.append(remote(piece, piece, s_z.at[i], r_z.at[i], line_peer(dz, 0)))
     for c in z_c:
         c.start()
     core_c = [remote(WC.at[mine, :, core], WC.at[mine, :, core], s_core.at[1], r_core.at[1], partner)]
@@ -286,10 +296,9 @@
     UPS[2] = 0.75 * wide[1] + 0.25 * bottom
     UPS[3] = 0.25 * wide[1] + 0.75 * bottom
 
-    your_lower = WC.at[yours, pl.ds(0, 4), core]
-    your_upper = WC.at[yours, pl.ds(4, 4), core]
-    remote(your_lower, your_lower, s_z.at[0], r_z.at[0], partner).wait_recv()
-    remote(your_upper, your_upper, s_z.at[1], r_z.at[1], partner).wait_recv()
+    for i in range(4):
+        piece = WC.at[yours, pl.ds(2 * i, 2), core]
+        remote(piece, piece, s_z.at[i], r_z.at[i], partner).wait_recv()
     core_c.append(
         remote(WC.at[yours, :, core], WC.at[yours, :, core], s_core.at[2], r_core.at[2], partner)
     )
@@ -320,43 +329,36 @@
         from_partner = WC.at[part, :, 1 - core]
         remote(from_partner, from_partner, s_core.at[1], r_core.at[1 if c is core_c[0] else 2],
                partner).wait_recv()
-    acc = None
-    for tap in range(3):
-        w = jnp.concatenate([WC[3 * tap + i].reshape(256, 256) for i in range(3)], 1)
-        term = jnp.dot(w, JS[:, COLS * tap : COLS * (tap + 2)], preferred_element_type=f32)
-        acc = term if acc is None else acc + term
-    CO[0] = acc[:, :COLS].astype(bf16)
-    CO[1] = acc[:, COLS:].astype(bf16)
-    line_src[1] = row_stats([acc[:, :COLS], acc[:, COLS:]])
-    line2 = send_line(1)
     xf = lax.rem(2 * xe + core, 4)
     kept = (xf == x) & (lax.div(xe, 2) == core)
-    row_c = []
-    for j in range(2):
-        is_self = kept & (yl == j)
-        c = remote(CO.at[j], R.at[img], s_row.at[j], r_row.at[img], (z, yh, lax.div(xe, 2), xf, j))
-        row_c.append((is_self, c))
-
-        @pl.when(is_self)
-        def _():
-            R[img] = CO[j]
-
-        @pl.when(jnp.logical_not(is_self))
-        def _():
-            c.start()
+    taps = [jnp.concatenate([WC[3 * tap + i].reshape(256, 256) for i in range(3)], 1) for tap in range(3)]
+    conv_rows, row_c = [], []
+    for step in range(2):
+        j = 1 - yl if step == 0 else yl
+        acc = None
+        for tap in range(3):
+            cols = pl.ds(pl.multiple_of(COLS * (tap + j), COLS), COLS)
+            term = jnp.dot(taps[tap], JS[:, cols], preferred_element_type=f32)
+            acc = term if acc is None else acc + term
+        conv_rows.append(acc)
+        CO[j] = acc.astype(bf16)
+        row_c.append(remote(CO.at[j], R.at[img], s_row.at[step], r_row.at[img],
+                            (z, yh, lax.div(xe, 2), xf, j)))
+    plane_src[1] = row_stats(conv_rows)
+    plane2 = send_plane(1, PLANE_OFF)
+    row_c[0].start()
+
+    @pl.when(kept)
+    def _():
+        R[img] = CO[yl]
+
+    @pl.when(jnp.logical_not(kept))
+    def _():
+        row_c[1].start()
 
     gain2, shift2, bias = param(2), param(3), param(4)
     bias_out[...] = bias
     mask_out[...] = WC[9].reshape(256, 256)
-    for c in line2:
-        c.wait_recv()
-    plane_src[1] = line_total(1)
-    plane2 = send_plane(1, PLANE_OFF)
-    for n in range(2):
-        @pl.when(jnp.logical_not(kept & (img == n)))
-        def _():
-            remote(R.at[n], R.at[n], s_row.at[n], r_row.at[n], partner).wait_recv()
-
     for c in plane2:
         c.wait_recv()
     mine_sum, other_sum = plane_src[1], None
@@ -366,20 +368,44 @@
             mine_sum = mine_sum + v
         else:
             other_sum = v if other_sum is None else other_sum + v
-    for image, total in ((img, mine_sum), (1 - img, other_sum)):
+    line_src2[...] = jnp.concatenate([mine_sum, other_sum], 0)
+    line2 = []
+    for k, o in enumerate(LINE_OFF):
+        c = remote(line_src2, line_dst2.at[k], s_line.at[1, k], r_line.at[1, k], line_peer(*o))
+        c.start()
+        line2.append(c)
+    for group in (latw_c, par_c, w_c, [latw_core], halo_c, coarse_halo, z_c, core_c, plane1, line1, plane2):
+        for c in group:
+            c.wait_send()
+    for is_self, *cs, _, _ in shares:
+        @pl.when(jnp.logical_not(is_self))
+        def _():
+            for c in cs:
+                c.wait_send()
+
+    row_c[0].wait_send()
+
+    @pl.when(jnp.logical_not(kept))
+    def _():
+        row_c[1].wait_send()
+
+    for n in range(2):
+        @pl.when(jnp.logical_not(kept & (img == n)))
+        def _():
+            remote(R.at[n], R.at[n], s_row.at[n], r_row.at[n], partner).wait_recv()
+
+    for c in line2:
+        c.wait_recv()
+    both = line_src2[...]
+    for k in range(len(LINE_OFF)):
+        both = both + line_dst2[k]
+    for image, total in ((img, both[0:1]), (1 - img, both[1:2])):
         a, b = scale_shift(total, gain2, shift2)
         act_out[image] = jnp.maximum(
             R[image].astype(f32) * jnp.concatenate([a] * 4, 1) + jnp.concatenate([b] * 4, 1), 0.0
         ).astype(bf16)
-    for group in (latw_c, par_c, w_c, [latw_core], halo_c, coarse_halo, z_c, core_c, plane1, plane2,
-                  line1, line2):
-        for c in group:
-            c.wait_send()
-    for is_self, *cs in shares + row_c:
-        @pl.when(jnp.logical_not(is_self))
-        def _():
-            for c in cs:
-                c.wait_send()
+    for c in line2:
+        c.wait_send()
 
 
 def log_probs_of(act, mask_w, bias, queries, out):
@@ -433,13 +459,15 @@
             V((2, D, COLS), bf16),
             V((2, 1, 128), f32),
             V((2, 15, 1, 128), f32),
-            V((2, 1, 128), f32),
-            V((2, 15, 1, 128), f32),
+            V((1, 1, 128), f32),
+            V((1, 15, 1, 128), f32),
+            V((2, 128), f32),
+            V((15, 2, 128), f32),
         ]
         + [dma((8,))] * 4
         + [dma((7,))] * 6
         + [dma((4,))] * 2
-        + [dma((2,))] * 2
+        + [dma((4,))] * 2
         + [dma((3,))] * 2
         + [dma((2, 15))] * 4
         + [dma((2,))] * 2,

time: 47.3 us -> 45.9 us (0.970); the launches traced: 46.4 us -> 45.8 us
  Pallas kernels: 46.4 us -> 45.8 us
    pallas_call x1, Pallas kernels: 44.5 us -> 44 us  [per_device(): pl.pallas_call(functools.partial(kernel, pixels), out_shape=(jax.ShapeDty...]
where the time goes in v4:
time: 45.9 us; the launch traced here: 45.8 us
  Pallas kernels  45.8 us (100%)
    pallas_call x1, Pallas kernels, per_device(): pl.pallas_call(functools.partial(kernel, pixels), out_shape=(jax.ShapeDty...  44 us
    pallas_call x1, Pallas kernels, per_device(): pl.pallas_call(log_probs_of, out_shape=jax.ShapeDtypeStruct((2, 800, 128)...  1.87 us

profile of v4, /device:TPU:1, one launch (start us, length us, event | category | flops | bytes accessed | tf_op | source)
XLA Modules:
  0.0 45.8 jit_solution(10162596513405076428)
XLA Ops:
  0.0 0.0 copy-start
  0.0 44.0 %merge.1 = (bf16[2,256,512]{2,1,0:T(8,128)(2,1)S(1)}, bf16[256,256]{1,0:T(8,128)(2,1)S(1)}, f32[256,128]{1,0:T(8,128)S(1)}) custom-call(bf16[384,512]{1,0:T(8,128)(2,1)} %bitcast.10, bf16[2,32,4,256]{3,2,1,0:T(4,128)(2,1)} %coarse_in.1, bf16[2,16,192]{2,1,0:T(8,128)(2,1)} %bitcast.12, bf16[1,32]{1,0:T(2,128)(2,1)} %bitcast.14, bf16[1,32]{1,0:T(2,128)(2,1)} %bitcast.15, ...), custom_call_target="tpu_custom_call" | custom-call | tf_op jit(solution)/shard_map/merge/pallas_call | solution.py:430
  44.0 0.0 copy-done
  44.0 1.9 %log_probs.1 = f32[2,800,128]{2,1,0:T(8,128)} custom-call(bf16[2,256,512]{2,1,0:T(8,128)(2,1)S(1)} %get-tuple-element.8.act, bf16[256,256]{1,0:T(8,128)(2,1)S(1)} %get-tuple-element.9.mask_w, f32[256,128]{1,0:T(8,128)S(1)} %get-tuple-element.10.bias, bf16[200,256]{1,0:T(8,128)(2,1)S(1)} %copy-done), custom_call_target="tpu_custom_call" | custom-call | tf_op jit(solution)/shard_map/log_probs/pallas_call | solution.py:484
Async XLA Ops:
  0.0 44.0 %copy-start = (bf16[200,256]{1,0:T(8,128)(2,1)S(1)}, bf16[200,256]{1,0:T(8,128)(2,1)}, u32[]{:S(2)}) copy-start(bf16[200,256]{1,0:T(8,128)(2,1)} %queries.1) | copy-start | bytes 307204

commit v5 on v4

--- a/solution.py
+++ b/solution.py
@@ -18,7 +18,7 @@
 f32, bf16 = jnp.float32, jnp.bfloat16
 epsilon = 1e-05
 
-CHAN_OFF = [(dx, dy) for dx in (2, 1, 3, 0) for dy in (1, 0) if (dx, dy) != (0, 0)]
+CHAN_OFF = [(dx, dy) for dx in (0, 1, 3, 2) for dy in (1, 0) if (dx, dy) != (0, 0)]
 PLANE_OFF = [
     (dx, dh, dl)
     for dx in (2, 1, 3, 0)
@@ -29,6 +29,7 @@
 SAME_OFF = [o for o in PLANE_OFF if o[1] == o[2]]
 LINE_OFF = [(dz, dc) for dz in (4, 3, 5, 2, 6, 1, 7, 0) for dc in (1, 0) if (dz, dc) != (0, 0)]
 DEST = [(0, 0, 1), (1, 1, 0), (0, 0, 0), (1, 1, 1), (0, 1, 1), (1, 0, 0), (0, 1, 0), (1, 0, 1)]
+PIECES = (0, 3, 1, 2)
 
 
 def kernel(
@@ -154,10 +155,6 @@
         def _():
             cc.start()
 
-    for c in w_c:
-        c.start()
-    for c in par_c:
-        c.start()
 
     def wait_shares(buf, width, send, recv):
         for s in range(8):
@@ -228,6 +225,10 @@
     latw_core.start()
     wait_shares(X, 2, s_fine, r_fine)
     latw_core.wait_recv()
+    for c in w_c:
+        c.start()
+    for c in par_c:
+        c.start()
     own_rows = [lateral_of(1), lateral_of(2)]
     LAT[1] = own_rows[0]
     LAT[2] = own_rows[1]
@@ -248,31 +249,42 @@
     for c in coarse_halo:
         c.start()
 
-    for c in w_c:
-        c.wait_recv()
     mine = pl.ds(5 * half, 5)
     yours = pl.ds(5 * (1 - half), 5)
     z_c = []
-    for i in range(4):
-        if i == 0:
-            dz = 1
-        elif i == 1:
-            dz = jnp.where((x == 0) & (yh == 1), 7, 1)
-        elif i == 2:
-            dz = jnp.where((x == 0) & (yh == 0), 1, 7)
-        else:
-            dz = 7
-        piece = WC.at[mine, pl.ds(2 * i, 2), core]
-        z_c.append(remote(piece, piece, s_z.at[i], r_z.at[i], line_peer(dz, 0)))
-    for c in z_c:
-        c.start()
-    core_c = [remote(WC.at[mine, :, core], WC.at[mine, :, core], s_core.at[1], r_core.at[1], partner)]
-    core_c[0].start()
-
+
+    def piece_of(part, i):
+        return WC.at[part, pl.ds(2 * lax.rem(x + PIECES[i], 4), 2), core]
+
+    def pass_piece(i):
+        for k, o in enumerate(CHAN_OFF):
+            if (o[0] + PIECES[i]) % 4 == 0:
+                w_c[k].wait_recv()
+        dz = (1, 7, 1, 7)[i]
+        c = remote(piece_of(mine, i), piece_of(mine, i), s_z.at[i], r_z.at[i], line_peer(dz, 0))
+        c.start()
+        z_c.append(c)
+
+    core_c = []
+
+    def take_piece(i):
+        piece = piece_of(yours, i)
+        remote(piece, piece, s_z.at[i], r_z.at[i], partner).wait_recv()
+        c = remote(piece, piece, s_core.at[2 + i], r_core.at[2 + i], partner)
+        c.start()
+        core_c.append(c)
+
+    pass_piece(0)
     for c in line1:
         c.wait_recv()
     plane_src[0] = line_total(0)
     plane1 = send_plane(0, SAME_OFF)
+
+    pass_piece(1)
+    pass_piece(2)
+    pass_piece(3)
+    core_mine = remote(WC.at[mine, :, core], WC.at[mine, :, core], s_core.at[1], r_core.at[1], partner)
+    core_mine.start()
 
     for c in par_c:
         c.wait_recv()
@@ -286,6 +298,8 @@
         c.wait_recv()
     LAT[0] = lateral_of(0)
     LAT[3] = lateral_of(3)
+    take_piece(0)
+    take_piece(1)
     for c in coarse_halo:
         c.wait_recv()
     wide = [jnp.dot(C[s].reshape(256, 256), widen, preferred_element_type=f32) for s in range(3)]
@@ -296,14 +310,8 @@
     UPS[2] = 0.75 * wide[1] + 0.25 * bottom
     UPS[3] = 0.25 * wide[1] + 0.75 * bottom
 
-    for i in range(4):
-        piece = WC.at[yours, pl.ds(2 * i, 2), core]
-        remote(piece, piece, s_z.at[i], r_z.at[i], partner).wait_recv()
-    core_c.append(
-        remote(WC.at[yours, :, core], WC.at[yours, :, core], s_core.at[2], r_core.at[2], partner)
-    )
-    core_c[1].start()
-
+    take_piece(2)
+    take_piece(3)
     for c in plane1:
         c.wait_recv()
     t = plane_src[0]
@@ -314,6 +322,7 @@
     a4 = jnp.concatenate([a] * 4, 1)
     b4 = jnp.concatenate([b] * 4, 1)
     lane = lax.broadcasted_iota(jnp.int32, (D, COLS), 1)
+    zero = jnp.zeros((), bf16)
     for s in range(4):
         j = LAT[s] * a4 + b4 + UPS[s]
         if s == 0:
@@ -321,14 +330,16 @@
         if s == 3:
             j = jnp.where(pair == 127, 0.0, j)
         cols = slice(COLS * s, COLS * (s + 1))
-        JS[0:256, cols] = jnp.where(lane == 0, 0.0, pltpu.roll(j, 1, 1)).astype(bf16)
-        JS[256:512, cols] = j.astype(bf16)
-        JS[512:768, cols] = jnp.where(lane == COLS - 1, 0.0, pltpu.roll(j, COLS - 1, 1)).astype(bf16)
-
-    for part, c in ((mine, core_c[0]), (yours, core_c[1])):
-        from_partner = WC.at[part, :, 1 - core]
-        remote(from_partner, from_partner, s_core.at[1], r_core.at[1 if c is core_c[0] else 2],
-               partner).wait_recv()
+        j = j.astype(bf16)
+        JS[0:256, cols] = jnp.where(lane == 0, zero, pltpu.roll(j, 1, 1))
+        JS[256:512, cols] = j
+        JS[512:768, cols] = jnp.where(lane == COLS - 1, zero, pltpu.roll(j, COLS - 1, 1))
+
+    whole = WC.at[mine, :, 1 - core]
+    remote(whole, whole, s_core.at[1], r_core.at[1], partner).wait_recv()
+    for i in range(4):
+        piece = WC.at[yours, pl.ds(2 * lax.rem(x + PIECES[i], 4), 2), 1 - core]
+        remote(piece, piece, s_core.at[2 + i], r_core.at[2 + i], partner).wait_recv()
     xf = lax.rem(2 * xe + core, 4)
     kept = (xf == x) & (lax.div(xe, 2) == core)
     taps = [jnp.concatenate([WC[3 * tap + i].reshape(256, 256) for i in range(3)], 1) for tap in range(3)]
@@ -374,7 +385,7 @@
         c = remote(line_src2, line_dst2.at[k], s_line.at[1, k], r_line.at[1, k], line_peer(*o))
         c.start()
         line2.append(c)
-    for group in (latw_c, par_c, w_c, [latw_core], halo_c, coarse_halo, z_c, core_c, plane1, line1, plane2):
+    for group in (latw_c, par_c, w_c, [latw_core], halo_c, coarse_halo, z_c, core_c, [core_mine], plane1, line1, plane2):
         for c in group:
             c.wait_send()
     for is_self, *cs, _, _ in shares:
@@ -468,7 +479,7 @@
         + [dma((7,))] * 6
         + [dma((4,))] * 2
         + [dma((4,))] * 2
-        + [dma((3,))] * 2
+        + [dma((6,))] * 2
         + [dma((2, 15))] * 4
         + [dma((2,))] * 2,
         compiler_params=pltpu.CompilerParams(

time: 45.9 us -> 45.1 us (0.983)
  Pallas kernels: 45.8 us -> 44.9 us
    pallas_call x1, Pallas kernels: 44 us -> 43.1 us  [per_device(): pl.pallas_call(functools.partial(kernel, pixels), out_shape=(jax.ShapeDty...]
where the time goes in v5:
time: 45.1 us; the launch traced here: 45 us
  Pallas kernels  44.9 us (100%)
    pallas_call x1, Pallas kernels, per_device(): pl.pallas_call(functools.partial(kernel, pixels), out_shape=(jax.ShapeDty...  43.1 us
    pallas_call x1, Pallas kernels, per_device(): pl.pallas_call(log_probs_of, out_shape=jax.ShapeDtypeStruct((2, 800, 128)...  1.87 us

profile of v5, /device:TPU:1, one launch (start us, length us, event | category | flops | bytes accessed | tf_op | source)
XLA Modules:
  0.0 45.0 jit_solution(10755841267260275262)
XLA Ops:
  0.0 0.0 copy-start
  0.0 43.1 %merge.1 = (bf16[2,256,512]{2,1,0:T(8,128)(2,1)S(1)}, bf16[256,256]{1,0:T(8,128)(2,1)S(1)}, f32[256,128]{1,0:T(8,128)S(1)}) custom-call(bf16[384,512]{1,0:T(8,128)(2,1)} %bitcast.10, bf16[2,32,4,256]{3,2,1,0:T(4,128)(2,1)} %coarse_in.1, bf16[2,16,192]{2,1,0:T(8,128)(2,1)} %bitcast.12, bf16[1,32]{1,0:T(2,128)(2,1)} %bitcast.14, bf16[1,32]{1,0:T(2,128)(2,1)} %bitcast.15, ...), custom_call_target="tpu_custom_call" | custom-call | tf_op jit(solution)/shard_map/merge/pallas_call | solution.py:441
  43.1 0.0 copy-done
  43.1 1.9 %log_probs.1 = f32[2,800,128]{2,1,0:T(8,128)} custom-call(bf16[2,256,512]{2,1,0:T(8,128)(2,1)S(1)} %get-tuple-element.8.act, bf16[256,256]{1,0:T(8,128)(2,1)S(1)} %get-tuple-element.9.mask_w, f32[256,128]{1,0:T(8,128)S(1)} %get-tuple-element.10.bias, bf16[200,256]{1,0:T(8,128)(2,1)S(1)} %copy-done), custom_call_target="tpu_custom_call" | custom-call | tf_op jit(solution)/shard_map/log_probs/pallas_call | solution.py:495
Async XLA Ops:
  0.0 43.1 %copy-start = (bf16[200,256]{1,0:T(8,128)(2,1)S(1)}, bf16[200,256]{1,0:T(8,128)(2,1)}, u32[]{:S(2)}) copy-start(bf16[200,256]{1,0:T(8,128)(2,1)} %queries.1) | copy-start | bytes 307204

commit v6 on v5

--- a/solution.py
+++ b/solution.py
@@ -49,7 +49,7 @@
     xe = fold(x, yh)
     img = lax.rem(yl + yh, 2)
     pair = (z * 2 + yh) * 8 + xe * 2 + core
-    half = lax.rem(z, 2)
+    half = lax.rem(z + yh, 2)
 
     def chan_peer(dx, dy, dc=0):
         return (z, yh, lax.rem(core + dc, 2), lax.rem(x + dx, 4), lax.rem(yl + dy, 2))
@@ -260,8 +260,8 @@
         for k, o in enumerate(CHAN_OFF):
             if (o[0] + PIECES[i]) % 4 == 0:
                 w_c[k].wait_recv()
-        dz = (1, 7, 1, 7)[i]
-        c = remote(piece_of(mine, i), piece_of(mine, i), s_z.at[i], r_z.at[i], line_peer(dz, 0))
+        dev = (line_peer(1, 0), line_peer(7, 0), plane_peer(0, 1, 1), line_peer(1 + 6 * yh, 0))[i]
+        c = remote(piece_of(mine, i), piece_of(mine, i), s_z.at[i], r_z.at[i], dev)
         c.start()
         z_c.append(c)
 

time: 45.1 us -> 45.1 us (level)
  no operation moved by 1% of the time
where the time goes in v6:
time: 45.1 us; the launch traced here: 45 us
  Pallas kernels  45 us (100%)
    pallas_call x1, Pallas kernels, per_device(): pl.pallas_call(functools.partial(kernel, pixels), out_shape=(jax.ShapeDty...  43.1 us
    pallas_call x1, Pallas kernels, per_device(): pl.pallas_call(log_probs_of, out_shape=jax.ShapeDtypeStruct((2, 800, 128)...  1.88 us

profile of v6, /device:TPU:1, one launch (start us, length us, event | category | flops | bytes accessed | tf_op | source)
XLA Modules:
  0.0 45.0 jit_solution(2269714330866772736)
XLA Ops:
  0.0 0.0 copy-start
  0.0 43.1 %merge.1 = (bf16[2,256,512]{2,1,0:T(8,128)(2,1)S(1)}, bf16[256,256]{1,0:T(8,128)(2,1)S(1)}, f32[256,128]{1,0:T(8,128)S(1)}) custom-call(bf16[384,512]{1,0:T(8,128)(2,1)} %bitcast.10, bf16[2,32,4,256]{3,2,1,0:T(4,128)(2,1)} %coarse_in.1, bf16[2,16,192]{2,1,0:T(8,128)(2,1)} %bitcast.12, bf16[1,32]{1,0:T(2,128)(2,1)} %bitcast.14, bf16[1,32]{1,0:T(2,128)(2,1)} %bitcast.15, ...), custom_call_target="tpu_custom_call" | custom-call | tf_op jit(solution)/shard_map/merge/pallas_call | solution.py:441
  43.2 0.0 copy-done
  43.2 1.9 %log_probs.1 = f32[2,800,128]{2,1,0:T(8,128)} custom-call(bf16[2,256,512]{2,1,0:T(8,128)(2,1)S(1)} %get-tuple-element.8.act, bf16[256,256]{1,0:T(8,128)(2,1)S(1)} %get-tuple-element.9.mask_w, f32[256,128]{1,0:T(8,128)S(1)} %get-tuple-element.10.bias, bf16[200,256]{1,0:T(8,128)(2,1)S(1)} %copy-done), custom_call_target="tpu_custom_call" | custom-call | tf_op jit(solution)/shard_map/log_probs/pallas_call | solution.py:495
Async XLA Ops:
  0.0 43.2 %copy-start = (bf16[200,256]{1,0:T(8,128)(2,1)S(1)}, bf16[200,256]{1,0:T(8,128)(2,1)}, u32[]{:S(2)}) copy-start(bf16[200,256]{1,0:T(8,128)(2,1)} %queries.1) | copy-start | bytes 307204

commit v7 on v6

--- a/solution.py
+++ b/solution.py
@@ -419,14 +419,20 @@
         c.wait_send()
 
 
-def log_probs_of(act, mask_w, bias, queries, out):
+def log_probs_of(act, mask_w, bias, queries, out, buf, sem):
     bias4 = jnp.concatenate([bias[...]] * 4, 1)
-    feat = (jnp.dot(mask_w[...], act[0], preferred_element_type=f32) + bias4).astype(bf16)
-    logits = jnp.dot(queries[...], feat, preferred_element_type=f32)
-    shifted = logits - jnp.max(logits, 0, keepdims=True)
-    res = shifted - jnp.log(jnp.sum(jnp.exp(shifted), 0, keepdims=True))
-    for k in range(4):
-        out[0, pl.ds(k, 200, stride=4), :] = res[:, 128 * k : 128 * (k + 1)]
+    copies = []
+    for n in range(2):
+        feat = (jnp.dot(mask_w[...], act[n], preferred_element_type=f32) + bias4).astype(bf16)
+        logits = jnp.dot(queries[...], feat, preferred_element_type=f32)
+        shifted = logits - jnp.max(logits, 0, keepdims=True)
+        res = shifted - jnp.log(jnp.sum(jnp.exp(shifted), 0, keepdims=True))
+        for k in range(4):
+            buf[n, pl.ds(k, 200, stride=4), :] = res[:, 128 * k : 128 * (k + 1)]
+        copies.append(pltpu.make_async_copy(buf.at[n], out.at[n], sem.at[n]))
+        copies[n].start()
+    for c in copies:
+        c.wait()
 
 
 def per_device(
@@ -495,14 +501,9 @@
     out = pl.pallas_call(
         log_probs_of,
         out_shape=jax.ShapeDtypeStruct((2, 800, 128), f32),
-        grid=(2,),
-        in_specs=[
-            pl.BlockSpec((1, D, COLS), lambda n: (n, 0, 0)),
-            pl.BlockSpec((D, D), lambda n: (0, 0)),
-            pl.BlockSpec((D, 128), lambda n: (0, 0)),
-            pl.BlockSpec((200, D), lambda n: (0, 0)),
-        ],
-        out_specs=pl.BlockSpec((1, 800, 128), lambda n: (n, 0, 0)),
+        in_specs=[pl.BlockSpec(memory_space=V)] * 4,
+        out_specs=pl.BlockSpec(memory_space=pl.ANY),
+        scratch_shapes=[V((2, 800, 128), f32), dma((2,))],
         compiler_params=pltpu.CompilerParams(vmem_limit_bytes=16 * 1024 * 1024),
         name="log_probs",
     )(act, mask_w, bias, queries)

time: 45.1 us -> 44.9 us (level)
  no operation moved by 1% of the time
where the time goes in v7:
time: 44.9 us; the launch traced here: 44.8 us
  Pallas kernels  44.8 us (100%)
    pallas_call x1, Pallas kernels, per_device(): pl.pallas_call(functools.partial(kernel, pixels), out_shape=(jax.ShapeDty...  43.1 us
    pallas_call x1, Pallas kernels, per_device(): pl.pallas_call(log_probs_of, out_shape=jax.ShapeDtypeStruct((2, 800, 128)...  1.64 us

profile of v7, /device:TPU:1, one launch (start us, length us, event | category | flops | bytes accessed | tf_op | source)
XLA Modules:
  0.0 44.8 jit_solution(1783799180970155442)
XLA Ops:
  0.0 0.0 copy-start
  0.0 43.1 %merge.1 = (bf16[2,256,512]{2,1,0:T(8,128)(2,1)S(1)}, bf16[256,256]{1,0:T(8,128)(2,1)S(1)}, f32[256,128]{1,0:T(8,128)S(1)}) custom-call(bf16[384,512]{1,0:T(8,128)(2,1)} %bitcast.10, bf16[2,32,4,256]{3,2,1,0:T(4,128)(2,1)} %coarse_in.1, bf16[2,16,192]{2,1,0:T(8,128)(2,1)} %bitcast.12, bf16[1,32]{1,0:T(2,128)(2,1)} %bitcast.14, bf16[1,32]{1,0:T(2,128)(2,1)} %bitcast.15, ...), custom_call_target="tpu_custom_call" | custom-call | tf_op jit(solution)/shard_map/merge/pallas_call | solution.py:447
  43.2 0.0 copy-done
  43.2 1.6 %log_probs.1 = f32[2,800,128]{2,1,0:T(8,128)} custom-call(bf16[2,256,512]{2,1,0:T(8,128)(2,1)S(1)} %get-tuple-element.8.act, bf16[256,256]{1,0:T(8,128)(2,1)S(1)} %get-tuple-element.9.mask_w, f32[256,128]{1,0:T(8,128)S(1)} %get-tuple-element.10.bias, bf16[200,256]{1,0:T(8,128)(2,1)S(1)} %copy-done), custom_call_target="tpu_custom_call" | custom-call | tf_op jit(solution)/shard_map/log_probs/pallas_call | solution.py:501
Async XLA Ops:
  0.0 43.2 %copy-start = (bf16[200,256]{1,0:T(8,128)(2,1)S(1)}, bf16[200,256]{1,0:T(8,128)(2,1)}, u32[]{:S(2)}) copy-start(bf16[200,256]{1,0:T(8,128)(2,1)} %queries.1) | copy-start | bytes 307204

commit v8 on v7

--- a/solution.py
+++ b/solution.py
@@ -28,7 +28,7 @@
 ]
 SAME_OFF = [o for o in PLANE_OFF if o[1] == o[2]]
 LINE_OFF = [(dz, dc) for dz in (4, 3, 5, 2, 6, 1, 7, 0) for dc in (1, 0) if (dz, dc) != (0, 0)]
-DEST = [(0, 0, 1), (1, 1, 0), (0, 0, 0), (1, 1, 1), (0, 1, 1), (1, 0, 0), (0, 1, 0), (1, 0, 1)]
+DEST = [(1, 0, 1), (0, 1, 0), (1, 1, 1), (0, 0, 0), (1, 0, 0), (0, 1, 1), (1, 1, 0), (0, 0, 1)]
 PIECES = (0, 3, 1, 2)
 
 
@@ -146,16 +146,6 @@
         pstage[j : j + 1, 0:32] = PV[j].astype(f32)
     PB[me] = pstage[...]
     WC[pl.ds(5 * half, 5), me, core] = WB[pl.ds(5 * half, 5), core]
-    for is_self, _, cc, image, pos in shares:
-        @pl.when(is_self)
-        def _():
-            C[1, me] = CB[image, pos]
-
-        @pl.when(jnp.logical_not(is_self))
-        def _():
-            cc.start()
-
-
     def wait_shares(buf, width, send, recv):
         for s in range(8):
             @pl.when(jnp.logical_not((s == me) & (lax.div(xe, 2) == core)))
@@ -223,6 +213,16 @@
         c.wait_recv()
     latw_core = remote(WL.at[:, core], WL.at[:, core], s_core.at[0], r_core.at[0], partner)
     latw_core.start()
+    for is_self, _, cc, image, pos in shares:
+        @pl.when(is_self)
+        def _():
+            C[1, me] = CB[image, pos]
+
+        @pl.when(jnp.logical_not(is_self))
+        def _():
+            cc.start()
+
+
     wait_shares(X, 2, s_fine, r_fine)
     latw_core.wait_recv()
     for c in w_c:
@@ -286,6 +286,8 @@
     core_mine = remote(WC.at[mine, :, core], WC.at[mine, :, core], s_core.at[1], r_core.at[1], partner)
     core_mine.start()
 
+    widened = lambda r: jnp.dot(C[r].reshape(256, 256), widen, preferred_element_type=f32)
+    own_wide = widened(1)
     for c in par_c:
         c.wait_recv()
     turned = jnp.transpose(jnp.concatenate([PB[...].reshape(64, 128), jnp.zeros((64, 128), f32)], 0))
@@ -302,7 +304,7 @@
     take_piece(1)
     for c in coarse_halo:
         c.wait_recv()
-    wide = [jnp.dot(C[s].reshape(256, 256), widen, preferred_element_type=f32) for s in range(3)]
+    wide = [widened(0), own_wide, widened(2)]
     top = jnp.where(pair == 0, wide[1], wide[0])
     bottom = jnp.where(pair == 127, wide[1], wide[2])
     UPS[0] = 0.75 * top + 0.25 * wide[1]

time: 44.9 us -> 44.9 us (level)
  no operation moved by 1% of the time
where the time goes in v8:
time: 44.9 us; the launch traced here: 44.8 us
  Pallas kernels  44.8 us (100%)
    pallas_call x1, Pallas kernels, per_device(): pl.pallas_call(functools.partial(kernel, pixels), out_shape=(jax.ShapeDty...  43.2 us
    pallas_call x1, Pallas kernels, per_device(): pl.pallas_call(log_probs_of, out_shape=jax.ShapeDtypeStruct((2, 800, 128)...  1.65 us

profile of v8, /device:TPU:1, one launch (start us, length us, event | category | flops | bytes accessed | tf_op | source)
XLA Modules:
  0.0 44.8 jit_solution(15758676917118804590)
XLA Ops:
  0.0 0.0 copy-start
  0.0 43.2 %merge.1 = (bf16[2,256,512]{2,1,0:T(8,128)(2,1)S(1)}, bf16[256,256]{1,0:T(8,128)(2,1)S(1)}, f32[256,128]{1,0:T(8,128)S(1)}) custom-call(bf16[384,512]{1,0:T(8,128)(2,1)} %bitcast.10, bf16[2,32,4,256]{3,2,1,0:T(4,128)(2,1)} %coarse_in.1, bf16[2,16,192]{2,1,0:T(8,128)(2,1)} %bitcast.12, bf16[1,32]{1,0:T(2,128)(2,1)} %bitcast.14, bf16[1,32]{1,0:T(2,128)(2,1)} %bitcast.15, ...), custom_call_target="tpu_custom_call" | custom-call | tf_op jit(solution)/shard_map/merge/pallas_call | solution.py:449
  43.2 0.0 copy-done
  43.2 1.6 %log_probs.1 = f32[2,800,128]{2,1,0:T(8,128)} custom-call(bf16[2,256,512]{2,1,0:T(8,128)(2,1)S(1)} %get-tuple-element.8.act, bf16[256,256]{1,0:T(8,128)(2,1)S(1)} %get-tuple-element.9.mask_w, f32[256,128]{1,0:T(8,128)S(1)} %get-tuple-element.10.bias, bf16[200,256]{1,0:T(8,128)(2,1)S(1)} %copy-done), custom_call_target="tpu_custom_call" | custom-call | tf_op jit(solution)/shard_map/log_probs/pallas_call | solution.py:503
Async XLA Ops:
  0.0 43.2 %copy-start = (bf16[200,256]{1,0:T(8,128)(2,1)S(1)}, bf16[200,256]{1,0:T(8,128)(2,1)}, u32[]{:S(2)}) copy-start(bf16[200,256]{1,0:T(8,128)(2,1)} %queries.1) | copy-start | bytes 307204

commit v9 on v8

--- a/solution.py
+++ b/solution.py
@@ -29,6 +29,7 @@
 SAME_OFF = [o for o in PLANE_OFF if o[1] == o[2]]
 LINE_OFF = [(dz, dc) for dz in (4, 3, 5, 2, 6, 1, 7, 0) for dc in (1, 0) if (dz, dc) != (0, 0)]
 DEST = [(1, 0, 1), (0, 1, 0), (1, 1, 1), (0, 0, 0), (1, 0, 0), (0, 1, 1), (1, 1, 0), (0, 0, 1)]
+PARTS = (pl.ds(0, 128), pl.ds(128, 128))
 PIECES = (0, 3, 1, 2)
 
 
@@ -355,19 +356,23 @@
             acc = term if acc is None else acc + term
         conv_rows.append(acc)
         CO[j] = acc.astype(bf16)
-        row_c.append(remote(CO.at[j], R.at[img], s_row.at[step], r_row.at[img],
-                            (z, yh, lax.div(xe, 2), xf, j)))
+        dev = (z, yh, lax.div(xe, 2), xf, j)
+        row_c.append([
+            remote(CO.at[j, part], R.at[img, part], s_row.at[step, h], r_row.at[img, h], dev)
+            for h, part in enumerate(PARTS)
+        ])
     plane_src[1] = row_stats(conv_rows)
     plane2 = send_plane(1, PLANE_OFF)
-    row_c[0].start()
-
     @pl.when(kept)
     def _():
         R[img] = CO[yl]
 
-    @pl.when(jnp.logical_not(kept))
-    def _():
-        row_c[1].start()
+    for h in range(len(PARTS)):
+        row_c[0][h].start()
+
+        @pl.when(jnp.logical_not(kept))
+        def _():
+            row_c[1][h].start()
 
     gain2, shift2, bias = param(2), param(3), param(4)
     bias_out[...] = bias
@@ -396,16 +401,19 @@
             for c in cs:
                 c.wait_send()
 
-    row_c[0].wait_send()
+    for c in row_c[0]:
+        c.wait_send()
 
     @pl.when(jnp.logical_not(kept))
     def _():
-        row_c[1].wait_send()
+        for c in row_c[1]:
+            c.wait_send()
 
     for n in range(2):
         @pl.when(jnp.logical_not(kept & (img == n)))
         def _():
-            remote(R.at[n], R.at[n], s_row.at[n], r_row.at[n], partner).wait_recv()
+            for h, part in enumerate(PARTS):
+                remote(R.at[n, part], R.at[n, part], s_row.at[n, h], r_row.at[n, h], partner).wait_recv()
 
     for c in line2:
         c.wait_recv()
@@ -489,7 +497,7 @@
         + [dma((4,))] * 2
         + [dma((6,))] * 2
         + [dma((2, 15))] * 4
-        + [dma((2,))] * 2,
+        + [dma((2, 2))] * 2,
         compiler_params=pltpu.CompilerParams(
             collective_id=0, has_side_effects=True, vmem_limit_bytes=40 * 1024 * 1024
         ),

time: 44.9 us -> 45 us (level)
  no operation moved by 1% of the time
where the time goes in v9:
time: 45 us; the launch traced here: 44.9 us
  Pallas kernels  44.9 us (100%)
    pallas_call x1, Pallas kernels, per_device(): pl.pallas_call(functools.partial(kernel, pixels), out_shape=(jax.ShapeDty...  43.2 us
    pallas_call x1, Pallas kernels, per_device(): pl.pallas_call(log_probs_of, out_shape=jax.ShapeDtypeStruct((2, 800, 128)...  1.65 us

profile of v9, /device:TPU:1, one launch (start us, length us, event | category | flops | bytes accessed | tf_op | source)
XLA Modules:
  0.0 44.9 jit_solution(16197510717996400347)
XLA Ops:
  0.0 0.0 copy-start
  0.0 43.2 %merge.1 = (bf16[2,256,512]{2,1,0:T(8,128)(2,1)S(1)}, bf16[256,256]{1,0:T(8,128)(2,1)S(1)}, f32[256,128]{1,0:T(8,128)S(1)}) custom-call(bf16[384,512]{1,0:T(8,128)(2,1)} %bitcast.10, bf16[2,32,4,256]{3,2,1,0:T(4,128)(2,1)} %coarse_in.1, bf16[2,16,192]{2,1,0:T(8,128)(2,1)} %bitcast.12, bf16[1,32]{1,0:T(2,128)(2,1)} %bitcast.14, bf16[1,32]{1,0:T(2,128)(2,1)} %bitcast.15, ...), custom_call_target="tpu_custom_call" | custom-call | tf_op jit(solution)/shard_map/merge/pallas_call | solution.py:457
  43.2 0.0 copy-done
  43.2 1.7 %log_probs.1 = f32[2,800,128]{2,1,0:T(8,128)} custom-call(bf16[2,256,512]{2,1,0:T(8,128)(2,1)S(1)} %get-tuple-element.8.act, bf16[256,256]{1,0:T(8,128)(2,1)S(1)} %get-tuple-element.9.mask_w, f32[256,128]{1,0:T(8,128)S(1)} %get-tuple-element.10.bias, bf16[200,256]{1,0:T(8,128)(2,1)S(1)} %copy-done), custom_call_target="tpu_custom_call" | custom-call | tf_op jit(solution)/shard_map/log_probs/pallas_call | solution.py:511
Async XLA Ops:
  0.0 43.2 %copy-start = (bf16[200,256]{1,0:T(8,128)(2,1)S(1)}, bf16[200,256]{1,0:T(8,128)(2,1)}, u32[]{:S(2)}) copy-start(bf16[200,256]{1,0:T(8,128)(2,1)} %queries.1) | copy-start | bytes 307204
